TPU v7x, 32 devices: a whole 2x2x4 slice. The times are simulated.
32 devices in a mesh: gx: 2 (over y), gy: 4 (over z), gz: 4 (over x, core).
Axes of the slice: x: 2, y: 2, z: 4, core: 2. Of those that a mesh axis runs over, the one named last changes fastest.
Arguments:
- velocity: float32 [8192, 3, 128], P(('gx', 'gy', 'gz')), may hold values from -6 to 6
- cell_index: int32 [8192, 128], P(('gx', 'gy', 'gz')), may hold values from 0 to 5804
- block_target: int32 [8192, 1], P(('gx', 'gy', 'gz')), may hold values from 0 to 31; in each aligned block of 256 rows (0 to 255, 256 to 511, ...) at most 12 rows name the same one
- rotation_axis: int32 [32, 32, 32], replicated, may hold values from 0 to 63
- grid_shift: int32 [3], replicated, may hold values from 0 to 31
Outputs:
- brick_velocity: float32 [32, 32, 12, 3, 128], P(('gx', 'gy', 'gz'))
- cell_flow: float32 [3, 8, 32, 512], P(None, 'gx', 'gy', 'gz')
Inputs may be any that keep to these rules, and one draw needn't show every extreme that they name: `block_target`: among the blocks that one device holds, no brick is named by more than 12 blocks, a bound that some block reaches.
All inputs are finite; a program needn't handle non-finite values.
Results may differ from a plain program's by a relative error of at most 0.0003.
Values sent between devices are 32-bit elements; how exact they have to be, the bound alone decides.
A program may use at most 64 MiB of HBM per device.

v0:
```python
import functools
import jax
import jax.numpy as jnp
from jax import lax
from jax.experimental import pallas as pl
from jax.experimental.pallas import tpu as pltpu
from jax.sharding import PartitionSpec as P

CX = 4
CY = 8
CZ = 128
NAX = 64
APER = 32
PLANES = (CX + 1) * (CY + 1)
HALF = 24
ROWS = 2 * HALF
WIDE = 2 * CZ
STEP = 8


angle_cosine = -0.6427876096865393
angle_sine = 0.766044443118978
highest = lax.Precision.HIGHEST


def with_halo(cells, sides, width):
    for axis, dim in sides:
        count = lax.axis_size(axis)
        head = lax.slice_in_dim(cells, 0, width, axis=dim)
        tail = lax.slice_in_dim(cells, cells.shape[dim] - width, cells.shape[dim], axis=dim)
        cells = jnp.concatenate(
            [
                lax.ppermute(tail, axis, [(i, (i + 1) % count) for i in range(count)]),
                cells,
                lax.ppermute(head, axis, [((i + 1) % count, i) for i in range(count)]),
            ],
            axis=dim,
        )
    return cells


def axis_table():
    counter = jnp.arange(NAX, dtype=jnp.float32) + 0.5
    height = 1.0 - 2.0 * counter / NAX
    radius = jnp.sqrt(jnp.maximum(1.0 - height * height, 0.0))
    turning = counter * 2.399963229728653
    return jnp.stack([radius * jnp.cos(turning), radius * jnp.sin(turning), height])


def rotate_about(direction, relative):
    inner_product = (
        direction[0] * relative[0] + direction[1] * relative[1] + direction[2] * relative[2]
    )
    crossed = [
        direction[1] * relative[2] - direction[2] * relative[1],
        direction[2] * relative[0] - direction[0] * relative[2],
        direction[0] * relative[1] - direction[1] * relative[0],
    ]
    return [
        relative[component] * angle_cosine
        + crossed[component] * angle_sine
        + direction[component] * inner_product * (1.0 - angle_cosine)
        for component in range(3)
    ]


def fold_rims(padded, dimension, length):
    inside = lax.slice_in_dim(padded, 1, length + 1, axis=dimension)
    lowest = lax.slice_in_dim(padded, 0, 1, axis=dimension)
    highest_rim = lax.slice_in_dim(padded, length + 1, length + 2, axis=dimension)
    position = lax.broadcasted_iota(jnp.int32, inside.shape, dimension)
    return (
        inside
        + jnp.where(position == 0, lowest, 0.0)
        + jnp.where(position == length - 1, highest_rim, 0.0)
    )


def lookup_table(rotation_axis, index_x, index_y, index_z):
    table = rotation_axis.astype(jnp.float32)
    pick_x = (index_x[:, None] == jnp.arange(APER, dtype=jnp.int32)[None, :]).astype(jnp.float32)
    pick_y = (index_y[:, None] == jnp.arange(APER, dtype=jnp.int32)[None, :]).astype(jnp.float32)
    pick_z = (index_z[:, None] == jnp.arange(APER, dtype=jnp.int32)[None, :]).astype(jnp.float32)
    section = jnp.einsum("xa,abc->xbc", pick_x, table, precision=highest)
    section = jnp.einsum("xbc,yb->xyc", section, pick_y, precision=highest)
    section = jnp.einsum("xyc,zc->xyz", section, pick_z, precision=highest)
    return (section + 0.5).astype(jnp.int32)


def pack_kernel(sizes, target_ref, velocity_ref, cell_ref, first_ref, second_ref, code_ref, count_ref):
    blocks = velocity_ref.shape[1]
    devices = count_ref.shape[0]
    cell = cell_ref[...]
    plane = (cell * 8129) >> 20
    depth = cell - plane * (CZ + 1)
    inner = depth < CZ
    row = jnp.where(inner, plane, PLANES)
    lane = jnp.where(inner, depth, plane)
    upper = row >= HALF
    code_ref[...] = jnp.where(
        upper, (row - HALF) * WIDE + CZ + lane, row * WIDE + lane
    ).astype(jnp.float32)
    for out_ref in (first_ref, second_ref):
        component = lax.broadcasted_iota(jnp.int32, out_ref.shape, 1)
        out_ref[...] = jnp.where(component == 3, -1.0, 0.0)

    def clear(d, carry):
        count_ref[d] = 0
        return carry

    lax.fori_loop(0, devices, clear, 0)

    def place(b, carry):
        target = target_ref[b]
        rank = count_ref[target]
        count_ref[target] = rank + 1

        def put(out_ref, slot):
            for component in range(3):
                out_ref[slot, component : component + 1, :] = velocity_ref[component, pl.ds(b, 1), :]
            out_ref[slot, 3:4, :] = code_ref[pl.ds(b, 1), :]

        @pl.when(rank < sizes[0])
        def early():
            put(first_ref, target * sizes[0] + rank)

        @pl.when(rank >= sizes[0])
        def late():
            put(second_ref, target * sizes[1] + rank - sizes[0])

        return carry

    lax.fori_loop(0, blocks, place, 0, unroll=4)


def code_onehots(labels):
    code = labels.astype(jnp.int32)
    row = code >> 8
    column = code & (WIDE - 1)
    width = labels.shape[1]
    by_row = lax.broadcasted_iota(jnp.int32, (HALF, width), 0) == row
    by_column = lax.broadcasted_iota(jnp.int32, (WIDE, width), 0) == column
    return by_row, by_column.astype(jnp.float32).astype(jnp.bfloat16)


def scatter_kernel(x_ref, before_ref, out_ref, total_ref, left_ref, right_ref):
    slots = x_ref.shape[0]
    for channel in range(4):
        total_ref[channel * HALF : (channel + 1) * HALF, 0:CZ] = before_ref[channel, 0:HALF, :]
        total_ref[channel * HALF : (channel + 1) * HALF, CZ:WIDE] = before_ref[channel, HALF:ROWS, :]
    total_ref[4 * HALF : 7 * HALF, :] = jnp.zeros((3 * HALF, WIDE), jnp.float32)

    def step(i, carry):
        for j in range(STEP):
            data = x_ref[i * STEP + j]
            by_row, by_column = code_onehots(data[3:4])
            right_ref[:, j * CZ : (j + 1) * CZ] = by_column
            moving = data[0:3]
            upper = moving.astype(jnp.bfloat16).astype(jnp.float32)
            lower = moving - upper
            parts = [jnp.where(by_row, 1.0, 0.0)]
            for source in (upper, lower):
                for component in range(3):
                    parts.append(jnp.where(by_row, source[component : component + 1], 0.0))
            left_ref[:, j * CZ : (j + 1) * CZ] = jnp.concatenate(parts, axis=0).astype(jnp.bfloat16)
        total_ref[...] += lax.dot_general(
            left_ref[...],
            right_ref[...],
            (((1,), (1,)), ((), ())),
            preferred_element_type=jnp.float32,
        )
        return carry

    lax.fori_loop(0, slots // STEP, step, 0)
    for channel in range(4):
        value = total_ref[channel * HALF : (channel + 1) * HALF, :]
        if channel > 0:
            value = value + total_ref[(channel + 3) * HALF : (channel + 4) * HALF, :]
        out_ref[channel, 0:HALF, :] = value[:, 0:CZ]
        out_ref[channel, HALF:ROWS, :] = value[:, CZ:WIDE]


def gather_kernel(sizes, first_ref, second_ref, table_ref, out_ref, held_ref):
    devices = out_ref.shape[2]
    groups = devices // STEP
    for channel in range(6):
        value = jnp.concatenate(
            [table_ref[channel, 0:HALF, :], table_ref[channel, HALF:ROWS, :]], axis=1
        )
        upper = value.astype(jnp.bfloat16)
        held_ref[channel * HALF : (channel + 1) * HALF, :] = upper
        held_ref[(channel + 6) * HALF : (channel + 7) * HALF, :] = (
            value - upper.astype(jnp.float32)
        ).astype(jnp.bfloat16)

    def read_from(x_ref, size, offset):
        def step(i, carry):
            rank = i // groups
            sender = (i % groups) * STEP
            blocks = [x_ref[(sender + j) * size + rank] for j in range(STEP)]
            picked = [[] for channel in range(6)]
            for j in range(0, STEP, 2):
                labels = jnp.concatenate([blocks[j][3:4], blocks[j + 1][3:4]], axis=1)
                by_row, by_column = code_onehots(labels)
                read = jnp.dot(held_ref[...], by_column, preferred_element_type=jnp.float32)
                for channel in range(6):
                    value = (
                        read[channel * HALF : (channel + 1) * HALF]
                        + read[(channel + 6) * HALF : (channel + 7) * HALF]
                    )
                    row = jnp.sum(jnp.where(by_row, value, 0.0), axis=0, keepdims=True)
                    picked[channel] += [row[:, 0:CZ], row[:, CZ:WIDE]]
            held = [jnp.concatenate(rows, axis=0) for rows in picked]
            own = [
                jnp.concatenate([block[c : c + 1] for block in blocks], axis=0) for c in range(4)
            ]
            relative = [own[c] - held[c] for c in range(3)]
            turned = rotate_about(held[3:], relative)
            place = pl.ds(pl.multiple_of(sender, STEP), STEP)
            for c in range(3):
                out_ref[offset + rank, c, place, :] = jnp.where(
                    own[3] >= 0.0, held[c] + turned[c], 0.0
                )
            return carry

        lax.fori_loop(0, size * groups, step, 0)

    read_from(first_ref, sizes[0], 0)
    read_from(second_ref, sizes[1], sizes[0])


def local_call(kernel, out_shape, in_spaces, scratch, operations):
    return pl.pallas_call(
        kernel,
        out_shape=[jax.ShapeDtypeStruct(shape, jnp.float32) for shape in out_shape],
        in_specs=[pl.BlockSpec(memory_space=space) for space in in_spaces],
        out_specs=[pl.BlockSpec(memory_space=pltpu.VMEM) for shape in out_shape],
        scratch_shapes=scratch,
        cost_estimate=pl.CostEstimate(
            flops=operations, bytes_accessed=1 << 20, transcendentals=0
        ),
    )


def to_rows(cells):
    main = cells[..., :CZ].reshape(-1, PLANES, CZ)
    rim = cells[..., CZ].reshape(-1, 1, PLANES)
    rim = jnp.pad(rim, ((0, 0), (0, ROWS - PLANES - 1), (0, CZ - PLANES)))
    return jnp.concatenate([main, rim], axis=1)


def shards(velocity, cell_index, block_target, rotation_axis, grid_shift):
    devices = lax.axis_size(("gx", "gy", "gz"))
    blocks = velocity.shape[0]
    block_rows = velocity.shape[2]
    capacity = 3 * blocks // (2 * devices)
    sizes = (capacity // 2, capacity - capacity // 2)
    packed = local_call(
        functools.partial(pack_kernel, sizes),
        [(devices * size, 4, block_rows) for size in sizes],
        (pltpu.SMEM, pltpu.VMEM, pltpu.VMEM),
        [pltpu.VMEM((blocks, block_rows), jnp.float32), pltpu.SMEM((devices,), jnp.int32)],
        1 << 20,
    )(block_target[:, 0], jnp.transpose(velocity, (1, 0, 2)), cell_index)
    arrived = []
    totals = jnp.zeros((4, ROWS, CZ), jnp.float32)
    for size, outgoing in zip(sizes, packed):
        arrived.append(
            lax.all_to_all(
                outgoing.reshape(devices, size, 4, block_rows),
                ("gx", "gy", "gz"),
                split_axis=0,
                concat_axis=0,
                tiled=True,
            ).reshape(devices * size, 4, block_rows)
        )
    for arriving in arrived:
        totals = local_call(
            scatter_kernel,
            [(4, ROWS, CZ)],
            (pltpu.VMEM, pltpu.VMEM),
            [
                pltpu.VMEM((7 * HALF, WIDE), jnp.float32),
                pltpu.VMEM((7 * HALF, STEP * CZ), jnp.bfloat16),
                pltpu.VMEM((WIDE, STEP * CZ), jnp.bfloat16),
            ],
            1 << 33,
        )(arriving, totals)[0]
    main = totals[:, :PLANES].reshape(4, CX + 1, CY + 1, CZ)
    rim = totals[:, PLANES, :PLANES].reshape(4, CX + 1, CY + 1, 1)
    partial_value = jnp.concatenate([main, rim], axis=3)
    folded = fold_rims(with_halo(partial_value, (("gx", 1),), 1), 1, CX + 1)
    folded = fold_rims(with_halo(folded, (("gy", 2),), 1), 2, CY + 1)
    folded = fold_rims(with_halo(folded, (("gz", 3),), 1), 3, CZ + 1)
    cell_means = folded[1:] / jnp.maximum(folded[0], 1.0)
    cell_flow = cell_means[:, :CX, :CY, :CZ]
    index_x = (
        (lax.axis_index("gx") * CX + jnp.arange(CX + 1, dtype=jnp.int32))
        % (CX * lax.axis_size("gx"))
        + grid_shift[0]
    ) % APER
    index_y = (
        (lax.axis_index("gy") * CY + jnp.arange(CY + 1, dtype=jnp.int32))
        % (CY * lax.axis_size("gy"))
        + grid_shift[1]
    ) % APER
    index_z = (
        (lax.axis_index("gz") * CZ + jnp.arange(CZ + 1, dtype=jnp.int32))
        % (CZ * lax.axis_size("gz"))
        + grid_shift[2]
    ) % APER
    picked = lookup_table(rotation_axis, index_x, index_y, index_z).reshape(-1)
    choose = (jnp.arange(NAX, dtype=jnp.int32)[:, None] == picked[None, :]).astype(jnp.float32)
    direction = jnp.dot(axis_table(), choose, precision=highest)
    table = jnp.concatenate(
        [cell_means, direction.reshape(3, CX + 1, CY + 1, CZ + 1)], axis=0
    )
    updated = local_call(
        functools.partial(gather_kernel, sizes),
        [(capacity, 3, devices, block_rows)],
        (pltpu.VMEM, pltpu.VMEM, pltpu.VMEM),
        [pltpu.VMEM((12 * HALF, WIDE), jnp.bfloat16)],
        1 << 33,
    )(*arrived, to_rows(table))[0]
    return (jnp.transpose(updated, (2, 0, 1, 3))[None], cell_flow)


def solution(mesh):
    return jax.shard_map(
        shards,
        mesh=mesh,
        in_specs=(
            P(("gx", "gy", "gz"), None, None),
            P(("gx", "gy", "gz"), None),
            P(("gx", "gy", "gz"), None),
            P(),
            P(),
        ),
        out_specs=(P(("gx", "gy", "gz"), None, None, None, None), P(None, "gx", "gy", "gz")),
        check_vma=False,
    )
```

profile of v0, /device:TPU:0, one launch (start us, length us, event | category | flops | bytes accessed | tf_op | source)
XLA Modules:
  0.0 95.4 jit_solution(16826655413395989124)
XLA Ops:
  0.7 7.1 %shard_map.68 = (f32[192,4,128]{2,1,0:T(4,128)}, f32[192,4,128]{2,1,0:T(4,128)}) custom-call(s32[256]{0:T(256)} %bitcast.64, f32[3,256,128]{2,1,0:T(8,128)} %bitcast.49, s32[256,128]{1,0:T(8,128)} %cell_ref.1), custom_call_target="tpu_custom_call" | custom-call | flops 1048576 | bytes 1048576 | tf_op jit(solution)/shard_map/pallas_call | solution.py:258
  7.8 7.3 %all-to-all-start = ((f32[32,6,4,128]{3,2,1,0:T(4,128)}), f32[32,6,4,128]{3,2,1,0:T(4,128)S(1)}, u32[]{:S(2)}, u32[]{:S(2)}) async-start(f32[32,6,4,128]{3,2,1,0:T(4,128)} %bitcast.48), calls=%async_computation | async-start | bytes 786432 | tf_op jit(solution)/shard_map/all_to_all | solution.py:269
  15.1 0.6 fusion.39
  15.8 0.7 and_select_fusion.4
  16.4 0.6 and_select_fusion.2
  17.0 0.6 fusion.3
  17.6 0.2 convolution_bitcast_fusion
  17.8 0.7 and_select_fusion
  18.5 0.2 fusion.1
  18.7 0.2 eq.115
  18.9 0.6 fusion
  19.5 8.7 %all-to-all-done = f32[32,6,4,128]{3,2,1,0:T(4,128)S(1)} async-done(((f32[32,6,4,128]{3,2,1,0:T(4,128)}), f32[32,6,4,128]{3,2,1,0:T(4,128)S(1)}, u32[]{:S(2)}, u32[]{:S(2)}) %all-to-all-start) | async-done | bytes 393248 | tf_op jit(solution)/shard_map/all_to_all | solution.py:269
  28.2 2.6 %all-to-all-start.1 = ((f32[32,6,4,128]{3,2,1,0:T(4,128)}), f32[32,6,4,128]{3,2,1,0:T(4,128)S(1)}, u32[]{:S(2)}, u32[]{:S(2)}) async-start(f32[32,6,4,128]{3,2,1,0:T(4,128)} %bitcast.4), calls=%async_computation.1 | async-start | bytes 786432 | tf_op jit(solution)/shard_map/all_to_all | solution.py:269
  30.8 0.6 broadcast_in_dim.76.before_ref
  31.5 11.9 %shard_map.69.before_ref = f32[4,48,128]{2,1,0:T(8,128)} custom-call(f32[192,4,128]{2,1,0:T(4,128)} %bitcast.44, f32[4,48,128]{2,1,0:T(8,128)} %broadcast_in_dim.76.before_ref), custom_call_target="tpu_custom_call" | custom-call | flops 8589934592 | bytes 1048576 | tf_op jit(solution)/shard_map/pallas_call | solution.py:278
  43.4 0.5 all-to-all-done.1
  43.9 0.8 copy-done.2
  44.7 11.9 %shard_map.70 = f32[4,48,128]{2,1,0:T(8,128)} custom-call(f32[192,4,128]{2,1,0:T(4,128)} %bitcast.46, f32[4,48,128]{2,1,0:T(8,128)} %shard_map.69.before_ref), custom_call_target="tpu_custom_call" | custom-call | flops 8589934592 | bytes 1048576 | tf_op jit(solution)/shard_map/pallas_call | solution.py:278
  56.6 0.7 slice_reduce_fusion
  57.3 0.1 reshape_squeeze.6
  57.4 0.2 copy.19
  57.6 0.9 copy.18
  58.6 1.2 %collective-permute-start = (f32[4,1,9,129]{3,0,2,1:T(4,128)S(1)}, f32[4,1,9,129]{3,0,2,1:T(4,128)S(1)}, u32[]{:S(2)}, u32[]{:S(2)}) collective-permute-start(f32[4,1,9,129]{3,0,2,1:T(4,128)S(1)} %get-tuple-element.14), channel_id=1, source_target_pairs={{0,16},{16,0},{1,17},{17,1},{2,18},{18,2},{3,19},{19,3},{4,20},{20... | collective-permute-start | bytes 55736 | tf_op jit(solution)/shard_map/ppermute | solution.py:33
  59.8 0.9 collective-permute-start.1
  60.7 2.3 %collective-permute-done = f32[4,1,9,129]{3,0,2,1:T(4,128)S(1)} collective-permute-done((f32[4,1,9,129]{3,0,2,1:T(4,128)S(1)}, f32[4,1,9,129]{3,0,2,1:T(4,128)S(1)}, u32[]{:S(2)}, u32[]{:S(2)}) %collective-permute-start) | collective-permute-done | bytes 18608 | tf_op jit(solution)/shard_map/ppermute | solution.py:33
  63.0 0.8 collective-permute-done.1
  63.8 0.1 fusion.6
  63.9 1.6 %collective-permute-start.2 = (f32[4,5,1,129]{3,0,2,1:T(4,128)S(1)}, f32[4,5,1,129]{3,0,2,1:T(4,128)S(1)}, u32[]{:S(2)}, u32[]{:S(2)}) collective-permute-start(f32[4,5,1,129]{3,0,2,1:T(4,128)S(1)} %get-tuple-element.12), channel_id=1, source_target_pairs={{0,4},{4,8},{8,12},{12,0},{1,5},{5,9},{9,13},{13,1},{2,6},{6,10},{... | collective-permute-start | bytes 30968 | tf_op jit(solution)/shard_map/ppermute | solution.py:33
  65.5 2.3 %collective-permute-start.3 = (f32[4,5,1,129]{3,0,2,1:T(4,128)S(1)}, f32[4,5,1,129]{3,0,2,1:T(4,128)S(1)}, u32[]{:S(2)}, u32[]{:S(2)}) collective-permute-start(f32[4,5,1,129]{3,0,2,1:T(4,128)S(1)} %get-tuple-element.13), channel_id=1, source_target_pairs={{4,0},{8,4},{12,8},{0,12},{5,1},{9,5},{13,9},{1,13},{6,2},{10,6},{... | collective-permute-start | bytes 30968 | tf_op jit(solution)/shard_map/ppermute | solution.py:35
  67.8 1.8 %collective-permute-done.2 = f32[4,5,1,129]{3,0,2,1:T(4,128)S(1)} collective-permute-done((f32[4,5,1,129]{3,0,2,1:T(4,128)S(1)}, f32[4,5,1,129]{3,0,2,1:T(4,128)S(1)}, u32[]{:S(2)}, u32[]{:S(2)}) %collective-permute-start.2) | collective-permute-done | bytes 10352 | tf_op jit(solution)/shard_map/ppermute | solution.py:33
  69.6 0.0 collective-permute-done.3
  69.6 0.2 select_add_fusion.1
  69.8 0.1 collective-permute-start.4
  69.9 1.7 %collective-permute-start.5 = (f32[4,5,9,1]{3,0,2,1:T(4,128)S(1)}, f32[4,5,9,1]{3,0,2,1:T(4,128)S(1)}, u32[]{:S(2)}, u32[]{:S(2)}) collective-permute-start(f32[4,5,9,1]{3,0,2,1:T(4,128)S(1)} %get-tuple-element.11), channel_id=1, source_target_pairs={{1,0},{2,1},{3,2},{0,3},{5,4},{6,5},{7,6},{4,7},{9,8},{10,9},{11,1... | collective-permute-start | bytes 2168 | tf_op jit(solution)/shard_map/ppermute | solution.py:35
  71.6 0.2 reshape.154
  71.8 0.1 copy.28
  71.9 1.9 %collective-permute-done.4 = f32[4,5,9,1]{3,0,2,1:T(4,128)S(1)} collective-permute-done((f32[4,5,9,1]{3,0,2,1:T(4,128)S(1)}, f32[4,5,9,1]{3,0,2,1:T(4,128)S(1)}, u32[]{:S(2)}, u32[]{:S(2)}) %collective-permute-start.4) | collective-permute-done | bytes 752 | tf_op jit(solution)/shard_map/ppermute | solution.py:33
  73.8 0.2 copy.20
  74.1 0.1 copy.21
  74.2 0.2 copy.22
  74.4 0.1 copy.23
  74.5 0.2 select_add_fusion
  74.8 0.1 slice_divide_fusion
  74.9 0.1 fusion.8
  75.1 0.1 copy.33
  75.2 0.6 copy.31
  75.9 0.7 select_maximum_fusion.table_ref
  76.6 18.8 %shard_map.71 = f32[12,3,32,128]{3,2,1,0:T(8,128)} custom-call(f32[192,4,128]{2,1,0:T(4,128)} %bitcast.45, f32[192,4,128]{2,1,0:T(4,128)} %bitcast.47, f32[6,48,128]{2,1,0:T(8,128)} %select_maximum_fusion.table_ref), custom_call_target="tpu_custom_call" | custom-call | flops 8589934592 | bytes 1048576 | tf_op jit(solution)/shard_map/pallas_call | solution.py:318
  (23 shorter events, 0.3 us)
Async XLA Ops:
  0.6 14.5 %copy-start.3 = (s32[3]{0:T(128)S(1)}, s32[3]{0:T(128)}, u32[]{:S(2)}) copy-start(s32[3]{0:T(128)} %param.9) | copy-start | bytes 40
  0.6 15.1 %copy-start = (s32[32,32,32]{2,1,0:T(8,128)S(1)}, s32[32,32,32]{2,1,0:T(8,128)}, u32[]{:S(2)}) copy-start(s32[32,32,32]{2,1,0:T(8,128)} %param.8) | copy-start | bytes 393220
  7.8 20.4 %all-to-all-start = ((f32[32,6,4,128]{3,2,1,0:T(4,128)}), f32[32,6,4,128]{3,2,1,0:T(4,128)S(1)}, u32[]{:S(2)}, u32[]{:S(2)}) async-start(f32[32,6,4,128]{3,2,1,0:T(4,128)} %bitcast.48), calls=%async_computation | async-start | bytes 786432 | tf_op jit(solution)/shard_map/all_to_all | solution.py:269
  28.2 3.3 %copy-start.1 = (f32[32,6,4,128]{3,2,1,0:T(4,128)}, f32[32,6,4,128]{3,2,1,0:T(4,128)S(1)}, u32[]{:S(2)}) copy-start(f32[32,6,4,128]{3,2,1,0:T(4,128)S(1)} %all-to-all-done) | copy-start | bytes 1179652
  28.2 15.7 %all-to-all-start.1 = ((f32[32,6,4,128]{3,2,1,0:T(4,128)}), f32[32,6,4,128]{3,2,1,0:T(4,128)S(1)}, u32[]{:S(2)}, u32[]{:S(2)}) async-start(f32[32,6,4,128]{3,2,1,0:T(4,128)} %bitcast.4), calls=%async_computation.1 | async-start | bytes 786432 | tf_op jit(solution)/shard_map/all_to_all | solution.py:269
  43.9 0.8 copy-start.2
  58.6 4.4 %collective-permute-start = (f32[4,1,9,129]{3,0,2,1:T(4,128)S(1)}, f32[4,1,9,129]{3,0,2,1:T(4,128)S(1)}, u32[]{:S(2)}, u32[]{:S(2)}) collective-permute-start(f32[4,1,9,129]{3,0,2,1:T(4,128)S(1)} %get-tuple-element.14), channel_id=1, source_target_pairs={{0,16},{16,0},{1,17},{17,1},{2,18},{18,2},{3,19},{19,3},{4,20},{20... | collective-permute-start | bytes 55736 | tf_op jit(solution)/shard_map/ppermute | solution.py:33
  59.8 4.0 %collective-permute-start.1 = (f32[4,1,9,129]{3,0,2,1:T(4,128)S(1)}, f32[4,1,9,129]{3,0,2,1:T(4,128)S(1)}, u32[]{:S(2)}, u32[]{:S(2)}) collective-permute-start(f32[4,1,9,129]{3,0,2,1:T(4,128)S(1)} %get-tuple-element.15), channel_id=1, source_target_pairs={{16,0},{0,16},{17,1},{1,17},{18,2},{2,18},{19,3},{3,19},{20,4},{4,... | collective-permute-start | bytes 55736 | tf_op jit(solution)/shard_map/ppermute | solution.py:35
  63.9 5.6 %collective-permute-start.2 = (f32[4,5,1,129]{3,0,2,1:T(4,128)S(1)}, f32[4,5,1,129]{3,0,2,1:T(4,128)S(1)}, u32[]{:S(2)}, u32[]{:S(2)}) collective-permute-start(f32[4,5,1,129]{3,0,2,1:T(4,128)S(1)} %get-tuple-element.12), channel_id=1, source_target_pairs={{0,4},{4,8},{8,12},{12,0},{1,5},{5,9},{9,13},{13,1},{2,6},{6,10},{... | collective-permute-start | bytes 30968 | tf_op jit(solution)/shard_map/ppermute | solution.py:33
  65.5 4.1 %collective-permute-start.3 = (f32[4,5,1,129]{3,0,2,1:T(4,128)S(1)}, f32[4,5,1,129]{3,0,2,1:T(4,128)S(1)}, u32[]{:S(2)}, u32[]{:S(2)}) collective-permute-start(f32[4,5,1,129]{3,0,2,1:T(4,128)S(1)} %get-tuple-element.13), channel_id=1, source_target_pairs={{4,0},{8,4},{12,8},{0,12},{5,1},{9,5},{13,9},{1,13},{6,2},{10,6},{... | collective-permute-start | bytes 30968 | tf_op jit(solution)/shard_map/ppermute | solution.py:35
  69.8 4.0 %collective-permute-start.4 = (f32[4,5,9,1]{3,0,2,1:T(4,128)S(1)}, f32[4,5,9,1]{3,0,2,1:T(4,128)S(1)}, u32[]{:S(2)}, u32[]{:S(2)}) collective-permute-start(f32[4,5,9,1]{3,0,2,1:T(4,128)S(1)} %get-tuple-element.10), channel_id=1, source_target_pairs={{0,1},{1,2},{2,3},{3,0},{4,5},{5,6},{6,7},{7,4},{8,9},{9,10},{10,1... | collective-permute-start | bytes 2168 | tf_op jit(solution)/shard_map/ppermute | solution.py:33
  69.9 4.3 %collective-permute-start.5 = (f32[4,5,9,1]{3,0,2,1:T(4,128)S(1)}, f32[4,5,9,1]{3,0,2,1:T(4,128)S(1)}, u32[]{:S(2)}, u32[]{:S(2)}) collective-permute-start(f32[4,5,9,1]{3,0,2,1:T(4,128)S(1)} %get-tuple-element.11), channel_id=1, source_target_pairs={{1,0},{2,1},{3,2},{0,3},{5,4},{6,5},{7,6},{4,7},{9,8},{10,9},{11,1... | collective-permute-start | bytes 2168 | tf_op jit(solution)/shard_map/ppermute | solution.py:35
where the time goes:
time: 96.6 us; the launch traced here: 95.4 us
  Pallas kernels  49.8 us (52%)
  starting transfers between devices  17.7 us (18%)
  waiting for transfers between devices  16 us (17%)
  local copies, waits for them, and re-layouts  5.96 us (6%)
  other arithmetic  3.59 us (4%)
  matrix products  1.53 us (2%)
    pallas_call x2, Pallas kernels, shards(): local_call(scatter_kernel, [(4, ROWS, CZ)], (pltpu.VMEM, pltpu.VMEM), [pl...  23.9 us
    pallas_call x1, Pallas kernels, shards(): local_call(functools.partial(gather_kernel, sizes), [(capacity, 3, device...  18.8 us
    all_to_all x2, starting transfers between devices, shards(): lax.all_to_all(outgoing.reshape(devices, size, 4, block_rows), ('gx', 'gy...  9.92 us
    all_to_all x2, waiting for transfers between devices, shards(): lax.all_to_all(outgoing.reshape(devices, size, 4, block_rows), ('gx', 'gy...  9.24 us
    pallas_call x1, Pallas kernels, shards(): local_call(functools.partial(pack_kernel, sizes), [(devices * size, 4, bl...  7.12 us
    ppermute x3, waiting for transfers between devices, with_halo(): lax.ppermute(tail, axis, [(i, (i + 1) % count) for i in range(count)])  5.97 us
    ppermute x3, starting transfers between devices, with_halo(): lax.ppermute(head, axis, [((i + 1) % count, i) for i in range(count)])  4.92 us
    ppermute x3, starting transfers between devices, with_halo(): lax.ppermute(tail, axis, [(i, (i + 1) % count) for i in range(count)])  2.84 us
  transfers between devices with their start and end apart: 8, of which 6 were waited for; matrix products, arithmetic and copies ran while one was open for 6% of the time, Pallas kernels for 12%

commit v1 on v0

v1 whole, which is shorter than its diff:
```python
import functools
import jax
import jax.numpy as jnp
import numpy as np
from jax import lax
from jax.experimental import pallas as pl
from jax.experimental.pallas import tpu as pltpu
from jax.sharding import PartitionSpec as P

CX = 4
CY = 8
CZ = 128
NAX = 64
APER = 32
EY = CY + 1
PLANES = (CX + 1) * EY
AXES = ("gx", "gy", "gz")
MESH_ID = pl.DeviceIdType.MESH

RIM = CY - 1
LOW = RIM + 1
HIGH = RIM + 2
SIDE = RIM + 3
INNER = SIDE + CX - 1
TILES = INNER + ((CX - 1) * (CY - 1) + 1) // 2
WIDE = 2 * CZ
STEP = 8

angle_cosine = -0.6427876096865393
angle_sine = 0.766044443118978


def axis_rows():
    counter = np.arange(NAX) + 0.5
    height = 1.0 - 2.0 * counter / NAX
    radius = np.sqrt(np.maximum(1.0 - height * height, 0.0))
    turning = counter * 2.399963229728653
    rows = np.zeros((8, 128), np.float32)
    rows[0, :NAX] = radius * np.cos(turning)
    rows[1, :NAX] = radius * np.sin(turning)
    rows[2, :NAX] = height
    return rows


def rotate_about(direction, relative):
    inner_product = (
        direction[0] * relative[0] + direction[1] * relative[1] + direction[2] * relative[2]
    )
    crossed = [
        direction[1] * relative[2] - direction[2] * relative[1],
        direction[2] * relative[0] - direction[0] * relative[2],
        direction[0] * relative[1] - direction[1] * relative[0],
    ]
    return [
        relative[component] * angle_cosine
        + crossed[component] * angle_sine
        + direction[component] * inner_product * (1.0 - angle_cosine)
        for component in range(3)
    ]


def take_lanes(values, index):
    return jnp.take_along_axis(values, index, axis=1, mode="promise_in_bounds")


def row_of_plane(ex, ey):
    static = isinstance(ex, int)
    where = (lambda c, a, b: a if c else b) if static else jnp.where
    inner = 2 * INNER + (ex - 1) * (CY - 1) + ey - 1
    last_x = ex == CX
    last_y = ey == CY
    half_x = where(last_x, 1, 0)
    half_y = where(last_y, 1, 0)
    corner = 2 * (LOW + half_y) + half_x
    side_x = 2 * (ey - 1) + half_x
    side_y = 2 * (SIDE + ex - 1) + half_y
    edge_x = (ex == 0) | last_x
    edge_y = (ey == 0) | last_y
    return where(
        edge_x, where(edge_y, corner, side_x), where(edge_y, side_y, inner)
    )


def position_codes(cell):
    plane = (cell * 8129) >> 20
    depth = cell - plane * (CZ + 1)
    ex = (plane * 57) >> 9
    ey = plane - ex * EY
    main = row_of_plane(ex, ey) * 128 + depth
    rim = 2 * RIM * 128 + plane
    return jnp.where(depth == CZ, rim, jnp.where(depth == 0, rim + 128, main))


def neighbours(sizes):
    steps = [(0, 1) if size == 2 else (0, 1, -1) for size in sizes]
    return [
        (dx, dy, dz)
        for dx in steps[0]
        for dy in steps[1]
        for dz in steps[2]
        if (dx, dy, dz) != (0, 0, 0)
    ]


def halo_tiles(step):
    if step[2] != 0:
        return RIM, LOW
    if step[0] != 0:
        return (RIM, SIDE) if step[1] != 0 else (0, SIDE)
    return RIM, INNER


def exchange_kernel(
    sizes,
    room,
    shift_ref,
    target_ref,
    velocity_ref,
    cell_ref,
    rotation_ref,
    recv_ref,
    table_ref,
    send_ref,
    total_ref,
    tile_ref,
    halo_ref,
    block_ref,
    plane_ref,
    kind_ref,
    send_sem,
    recv_sem,
    halo_send_sem,
    halo_recv_sem,
):
    nx, ny, nz = sizes
    devices = nx * ny * nz
    blocks = velocity_ref.shape[1]
    per = 4 * room
    place = tuple(lax.axis_index(axis) for axis in AXES)
    me = (place[0] * ny + place[1]) * nz + place[2]

    def away(k, sign):
        ox, oy, oz = k // (ny * nz), k // nz % ny, k % nz
        there = (
            (place[0] + sign * ox + nx) % nx,
            (place[1] + sign * oy + ny) % ny,
            (place[2] + sign * oz + nz) % nz,
        )
        return there, (there[0] * ny + there[1]) * nz + there[2]

    barrier = pltpu.get_barrier_semaphore()

    def greet(k, carry):
        there, number = away(k, 1)
        pl.semaphore_signal(barrier, inc=1, device_id=there, device_id_type=MESH_ID)
        return carry

    lax.fori_loop(1, devices, greet, 0)

    target = target_ref[...]
    named = (lax.broadcasted_iota(jnp.int32, (devices, blocks), 0) == target).astype(jnp.float32)
    earlier = (
        lax.broadcasted_iota(jnp.int32, (blocks, blocks), 0)
        < lax.broadcasted_iota(jnp.int32, (blocks, blocks), 1)
    ).astype(jnp.float32)
    before = jnp.dot(
        named.astype(jnp.bfloat16), earlier.astype(jnp.bfloat16), preferred_element_type=jnp.float32
    )
    rank = jnp.sum(named * before, axis=0, keepdims=True).astype(jnp.int32)
    slot = target * room + rank
    chosen = (
        (lax.broadcasted_iota(jnp.int32, (devices * room, blocks), 0) == slot)
        .astype(jnp.float32)
        .astype(jnp.bfloat16)
    )
    codes = position_codes(cell_ref[...]).astype(jnp.float32)
    for channel in range(4):
        left = codes if channel == 0 else velocity_ref[channel - 1]
        placed = None
        for part in range(3):
            upper = left.astype(jnp.bfloat16)
            moved = jnp.dot(chosen, upper, preferred_element_type=jnp.float32)
            placed = moved if placed is None else placed + moved
            left = left - upper.astype(jnp.float32)
        send_ref[pl.ds(channel, devices * room, stride=4), :] = placed

    lane = lax.broadcasted_iota(jnp.int32, (APER, 128), 1)
    depth_index = (lane + place[2] * CZ + shift_ref[2]) % APER
    for ex in range(CX + 1):
        index_x = ((place[0] * CX + ex) % (CX * nx) + shift_ref[0]) % APER
        layer = rotation_ref[index_x].astype(jnp.float32)
        layer = jnp.concatenate([layer] * (128 // APER), axis=1)
        block_ref[ex * APER : (ex + 1) * APER, :] = take_lanes(layer, depth_index)
        for ey in range(EY):
            index_y = ((place[1] * CY + ey) % (CY * ny) + shift_ref[1]) % APER
            row = block_ref[pl.ds(ex * APER + index_y, 1), :]
            plane_ref[ex * EY + ey : ex * EY + ey + 1, :] = row
            at = row_of_plane(ex, ey)
            kind_ref[at // 2, at % 2 : at % 2 + 1, :] = row
    planes = plane_ref[0 : 8 * (PLANES // 8 + 1), :]
    sublane = lax.broadcasted_iota(jnp.int32, planes.shape, 0)
    lanes = lax.broadcasted_iota(jnp.int32, planes.shape, 1)
    first = take_lanes(planes, jnp.zeros(planes.shape, jnp.int32))
    rim_kind = jnp.sum(
        jnp.where((sublane == lanes) & (sublane < PLANES), first, 0.0), axis=0, keepdims=True
    )
    kind_ref[RIM, 0:1, :] = rim_kind
    kind_ref[RIM, 1:2, :] = rim_kind
    kind_ref[TILES - 1, 1:2, :] = jnp.zeros((1, 128), jnp.float32)

    pl.semaphore_wait(barrier, devices - 1)

    def outgoing(k):
        there, number = away(k, 1)
        return pltpu.make_async_remote_copy(
            src_ref=send_ref.at[pl.ds(pl.multiple_of(number * per, 8), per), :],
            dst_ref=recv_ref.at[pl.ds(pl.multiple_of(me * per, 8), per), :],
            send_sem=send_sem.at[k],
            recv_sem=recv_sem.at[k],
            device_id=there,
            device_id_type=MESH_ID,
        )

    def start(k, carry):
        outgoing(k).start()
        return carry

    lax.fori_loop(1, devices, start, 0)
    own = pl.ds(pl.multiple_of(me * per, 8), per)
    recv_ref[own, :] = send_ref[own, :]
    total_ref[...] = jnp.zeros(total_ref.shape, jnp.float32)
    half = lax.broadcasted_iota(jnp.int32, (8, 128), 0)

    def add_sender(k, carry):
        _, number = away(k, -1)
        base = pl.multiple_of(number * per, 8)

        @pl.when(k > 0)
        def arrived():
            pltpu.make_async_remote_copy(
                src_ref=recv_ref.at[pl.ds(base, per), :],
                dst_ref=recv_ref.at[pl.ds(base, per), :],
                send_sem=send_sem.at[k],
                recv_sem=recv_sem.at[k],
                device_id=place,
                device_id_type=MESH_ID,
            ).wait_recv()

        by_row = lax.broadcasted_iota(jnp.int32, (8 * TILES, 128), 0) >> 3
        by_column = lax.broadcasted_iota(jnp.int32, (WIDE, 128), 0)
        lefts, rights = [], []
        for pair in range(room // 2):
            data = recv_ref[pl.ds(base + 8 * pair, 8), :]
            upper = data.astype(jnp.bfloat16).astype(jnp.float32)
            lower = data - upper
            whole = data.astype(jnp.int32)
            for which in range(2):
                if which == 0:
                    values = jnp.where(half < 4, upper, pltpu.roll(lower, 4, 0))
                else:
                    values = jnp.where(half < 4, pltpu.roll(upper, 4, 0), lower)
                values = jnp.where(half == 0, 1.0, jnp.where(half == 4, 0.0, values))
                code = whole[4 * which : 4 * which + 1]
                tiled = jnp.concatenate([values] * TILES, axis=0)
                lefts.append(jnp.where(by_row == code >> 8, tiled, 0.0).astype(jnp.bfloat16))
                rights.append(
                    (by_column == (code & (WIDE - 1))).astype(jnp.float32).astype(jnp.bfloat16)
                )
        middle = room // 2
        for part, span in enumerate((slice(0, middle), slice(middle, room))):
            total_ref[part] += lax.dot_general(
                jnp.concatenate(lefts[span], axis=1),
                jnp.concatenate(rights[span], axis=1),
                (((1,), (1,)), ((), ())),
                preferred_element_type=jnp.float32,
            )
        return carry

    lax.fori_loop(0, devices, add_sender, 0)

    for tile in range(TILES):
        rows = pl.ds(8 * tile, 8)
        value = total_ref[0, rows, :] + total_ref[1, rows, :]
        value = value + pltpu.roll(value, 4, 0)
        tile_ref[tile] = jnp.where(half < 4, value[:, :CZ], value[:, CZ:])

    steps = neighbours(sizes)

    def slot_of(step):
        return steps.index(
            tuple(abs(d) if size == 2 else d for d, size in zip(step, sizes))
        )

    copies = []
    for step in steps:
        low, high = halo_tiles(step)
        there = tuple((p + d + size) % size for p, d, size in zip(place, step, sizes))
        landing = slot_of(tuple(-d for d in step))
        copies.append(
            pltpu.make_async_remote_copy(
                src_ref=tile_ref.at[low:high],
                dst_ref=halo_ref.at[landing, 0 : high - low],
                send_sem=halo_send_sem.at[slot_of(step)],
                recv_sem=halo_recv_sem.at[landing],
                device_id=there,
                device_id_type=MESH_ID,
            )
        )
    for copy in copies:
        copy.start()

    def sent(k, carry):
        outgoing(k).wait_send()
        return carry

    lax.fori_loop(1, devices, sent, 0)
    for copy in copies:
        copy.wait()

    def got(step, tile):
        low, high = halo_tiles(step)
        return halo_ref[slot_of(step), tile - low]

    def turned(step, tile):
        return pltpu.roll(got(step, tile), 4, 0)

    def both(low, high):
        return jnp.where(half < 4, low, high)

    lane = lax.broadcasted_iota(jnp.int32, (8, 128), 1)
    plane_x = (lane * 57) >> 9
    plane_y = lane - plane_x * EY

    def rim(dx, dy):
        own_rim = tile_ref[RIM] if (dx, dy) == (0, 0) else got((dx, dy, 0), RIM)
        return own_rim + both(turned((dx, dy, 1), RIM), turned((dx, dy, -1), RIM))

    for tile in range(TILES):
        value = tile_ref[tile]
        if tile < RIM or tile in (LOW, HIGH):
            value = value + both(turned((-1, 0, 0), tile), turned((1, 0, 0), tile))
        if tile in (LOW, HIGH):
            dy, other = (-1, HIGH) if tile == LOW else (1, LOW)
            value = value + got((0, dy, 0), other)
            value = value + both(turned((-1, dy, 0), other), turned((1, dy, 0), other))
        if SIDE <= tile < INNER:
            value = value + both(turned((0, -1, 0), tile), turned((0, 1, 0), tile))
        if tile == RIM:
            value = rim(0, 0)
            for dx in (-1, 0, 1):
                for dy in (-1, 0, 1):
                    if (dx, dy) == (0, 0):
                        continue
                    inside = lane < PLANES
                    if dx != 0:
                        inside = inside & (plane_x == (CX if dx > 0 else 0))
                    if dy != 0:
                        inside = inside & (plane_y == (CY if dy > 0 else 0))
                    moved = pltpu.roll(rim(dx, dy), (dx * CX * EY + dy * CY) % 128, 1)
                    value = value + jnp.where(inside, moved, 0.0)
        count = both(
            jnp.broadcast_to(value[0:1], (8, 128)), jnp.broadcast_to(value[4:5], (8, 128))
        )
        mean = value / jnp.maximum(count, 1.0)
        kind = both(
            jnp.broadcast_to(kind_ref[tile, 0:1, :], (8, 128)),
            jnp.broadcast_to(kind_ref[tile, 1:2, :], (8, 128)),
        )
        table_ref[8 * tile : 8 * tile + 8, :] = jnp.where(half % 4 == 0, kind, mean)


def update_kernel(slots, room, recv_ref, table_ref, axis_ref, out_ref, flow_ref, held_ref):
    devices = out_ref.shape[2]
    per = 4 * room
    groups = devices // STEP
    for channel in range(4):
        value = jnp.concatenate(
            [
                table_ref[pl.ds(channel, TILES, stride=8), :],
                table_ref[pl.ds(channel + 4, TILES, stride=8), :],
            ],
            axis=1,
        )
        upper = value.astype(jnp.bfloat16)
        held_ref[channel * TILES : (channel + 1) * TILES, :] = upper
        if channel > 0:
            held_ref[(channel + 3) * TILES : (channel + 4) * TILES, :] = (
                value - upper.astype(jnp.float32)
            ).astype(jnp.bfloat16)

    sublane = lax.broadcasted_iota(jnp.int32, (CY, 128), 0)
    lane = lax.broadcasted_iota(jnp.int32, (CY, 128), 1)
    for component in range(3):
        rim = table_ref[8 * RIM + 5 + component : 8 * RIM + 6 + component, :]
        rim = jnp.broadcast_to(rim, (CY, 128))
        for ex in range(CX):
            rows = []
            for ey in range(CY):
                at = 4 * row_of_plane(ex, ey) + 1 + component
                rows.append(table_ref[at : at + 1, :])
            flow = jnp.concatenate(rows, axis=0)
            edge = take_lanes(rim, sublane + ex * EY)
            flow_ref[component, ex] = jnp.where(lane == 0, edge, flow)

    by_row = lax.broadcasted_iota(jnp.int32, (TILES, 2 * 128), 0)
    by_column = lax.broadcasted_iota(jnp.int32, (WIDE, 2 * 128), 0)

    def step(i, carry):
        rank = i // groups
        sender = (i % groups) * STEP
        blocks = [
            recv_ref[pl.ds((sender + j) * per + 4 * rank, 4), :] for j in range(STEP)
        ]
        picked = [[] for channel in range(4)]
        for j in range(0, STEP, 2):
            code = jnp.concatenate([blocks[j][0:1], blocks[j + 1][0:1]], axis=1).astype(jnp.int32)
            onehot = (by_column == (code & (WIDE - 1))).astype(jnp.float32).astype(jnp.bfloat16)
            read = jnp.dot(held_ref[...], onehot, preferred_element_type=jnp.float32)
            here = by_row == code >> 8
            for channel in range(4):
                value = read[channel * TILES : (channel + 1) * TILES]
                if channel > 0:
                    value = value + read[(channel + 3) * TILES : (channel + 4) * TILES]
                row = jnp.sum(jnp.where(here, value, 0.0), axis=0, keepdims=True)
                picked[channel] += [row[:, :128], row[:, 128:]]
        held = [jnp.concatenate(rows, axis=0) for rows in picked]
        own = [jnp.concatenate([block[c : c + 1] for block in blocks], axis=0) for c in range(4)]
        kind = held[0].astype(jnp.int32)
        direction = [
            take_lanes(jnp.broadcast_to(axis_ref[c : c + 1, :], (STEP, 128)), kind)
            for c in range(3)
        ]
        relative = [own[c + 1] - held[c + 1] for c in range(3)]
        turned = rotate_about(direction, relative)
        there = pl.ds(pl.multiple_of(sender, STEP), STEP)
        for c in range(3):
            out_ref[rank, c, there, :] = held[c + 1] + turned[c]
        return carry

    lax.fori_loop(0, slots * groups, step, 0)


def shards(velocity, cell_index, block_target, rotation_axis, grid_shift):
    sizes = tuple(lax.axis_size(axis) for axis in AXES)
    devices = sizes[0] * sizes[1] * sizes[2]
    blocks = velocity.shape[0]
    lanes = velocity.shape[2]
    slots = 3 * blocks // (2 * devices)
    room = slots + slots % 2
    count = len(neighbours(sizes))
    vmem = pl.BlockSpec(memory_space=pltpu.VMEM)
    arrived, table = pl.pallas_call(
        functools.partial(exchange_kernel, sizes, room),
        out_shape=[
            jax.ShapeDtypeStruct((devices * room * 4, lanes), jnp.float32),
            jax.ShapeDtypeStruct((8 * TILES, lanes), jnp.float32),
        ],
        in_specs=[pl.BlockSpec(memory_space=pltpu.SMEM), vmem, vmem, vmem, vmem],
        out_specs=[vmem, vmem],
        scratch_shapes=[
            pltpu.VMEM((devices * room * 4, lanes), jnp.float32),
            pltpu.VMEM((2, 8 * TILES, WIDE), jnp.float32),
            pltpu.VMEM((TILES, 8, lanes), jnp.float32),
            pltpu.VMEM((count, SIDE, 8, lanes), jnp.float32),
            pltpu.VMEM(((CX + 1) * APER, lanes), jnp.float32),
            pltpu.VMEM((8 * (PLANES // 8 + 1), lanes), jnp.float32),
            pltpu.VMEM((TILES, 8, lanes), jnp.float32),
            pltpu.SemaphoreType.DMA((devices,)),
            pltpu.SemaphoreType.DMA((devices,)),
            pltpu.SemaphoreType.DMA((count,)),
            pltpu.SemaphoreType.DMA((count,)),
        ],
        compiler_params=pltpu.CompilerParams(collective_id=0, has_side_effects=True),
        cost_estimate=pl.CostEstimate(flops=1 << 33, bytes_accessed=1 << 21, transcendentals=0),
    )(
        grid_shift,
        block_target.reshape(1, blocks),
        jnp.transpose(velocity, (1, 0, 2)),
        cell_index,
        rotation_axis,
    )
    updated, flow = pl.pallas_call(
        functools.partial(update_kernel, slots, room),
        out_shape=[
            jax.ShapeDtypeStruct((slots, 3, devices, lanes), jnp.float32),
            jax.ShapeDtypeStruct((3, CX, CY, CZ), jnp.float32),
        ],
        in_specs=[vmem, vmem, vmem],
        out_specs=[vmem, vmem],
        scratch_shapes=[pltpu.VMEM((7 * TILES, WIDE), jnp.bfloat16)],
        cost_estimate=pl.CostEstimate(flops=1 << 33, bytes_accessed=1 << 21, transcendentals=0),
    )(arrived, table, jnp.asarray(axis_rows()))
    return (jnp.transpose(updated, (2, 0, 1, 3))[None], flow)


def solution(mesh):
    return jax.shard_map(
        shards,
        mesh=mesh,
        in_specs=(
            P(AXES, None, None),
            P(AXES, None),
            P(AXES, None),
            P(),
            P(),
        ),
        out_specs=(P(AXES, None, None, None, None), P(None, "gx", "gy", "gz")),
        check_vma=False,
    )
```

time: 96.6 us -> 56.9 us (0.59); the launches traced: 95.4 us -> 56.7 us
  starting transfers between devices: 17.7 us -> 0 us
  waiting for transfers between devices: 16 us -> 0 us
  Pallas kernels: 49.8 us -> 56.1 us
  local copies, waits for them, and re-layouts: 5.96 us -> 0 us
  other arithmetic: 3.59 us -> 0 us
  matrix products: 1.53 us -> 0 us
    all_to_all x2 -> x0, starting transfers between devices: 9.92 us -> none  [shards(): lax.all_to_all(outgoing.reshape(devices, size, 4, block_rows), ('gx', 'gy...]
    all_to_all x2 -> x0, waiting for transfers between devices: 9.24 us -> none  [shards(): lax.all_to_all(outgoing.reshape(devices, size, 4, block_rows), ('gx', 'gy...]
    ppermute x6 -> x0, starting transfers between devices: 7.76 us -> none  [the longest x3 4.92 us: with_halo(): lax.ppermute(head, axis, [((i + 1) % count, i) for i in range(count)])]
    ppermute x6 -> x0, waiting for transfers between devices: 6.72 us -> none  [the longest x3 5.97 us: with_halo(): lax.ppermute(tail, axis, [(i, (i + 1) % count) for i in range(count)])]
    pallas_call x4 -> x2, Pallas kernels: 49.8 us -> 56.1 us  [the longest x1 38.2 us: shards(): pl.pallas_call(functools.partial(exchange_kernel, sizes, room), out_shape...]
    slice x6 -> x0, local copies, waits for them, and re-layouts: 2.33 us -> none  [the longest x1 0.93 us: shards(): main = totals[:, :PLANES].reshape(4, CX + 1, CY + 1, CZ)]
    select_n x3 -> x0, other arithmetic: 1.91 us -> none  [the longest x1 0.67 us: shards(): ((lax.axis_index('gz') * CZ + jnp.arange(CZ + 1, dtype=jnp.int32)) % (CZ...]
    dot_general x4 -> x0, matrix products: 1.53 us -> none  [the longest x1 0.59 us: lookup_table(): section = jnp.einsum('xa,abc->xbc', pick_x, table, precision=highest)]
  transfers between devices with their start and end apart: 8 -> 0, of which waited for: 6 -> 0; matrix products, arithmetic and copies ran while one was open for 6% -> 0% of each run, Pallas kernels for 12% -> 0%
where the time goes in v1:
time: 56.9 us; the launch traced here: 56.7 us
  Pallas kernels  56.1 us (99%)
  between operations  0.64 us (1%)
    pallas_call x1, Pallas kernels, shards(): pl.pallas_call(functools.partial(exchange_kernel, sizes, room), out_shape...  38.2 us
    pallas_call x1, Pallas kernels, shards(): pl.pallas_call(functools.partial(update_kernel, slots, room), out_shape=[...  17.9 us

profile of v1, /device:TPU:0, one launch (start us, length us, event | category | flops | bytes accessed | tf_op | source)
XLA Modules:
  0.0 56.7 jit_solution(7835792983412179375)
XLA Ops:
  0.6 38.2 %shard_map.77 = (f32[1536,128]{1,0:T(8,128)}, f32[192,128]{1,0:T(8,128)}) custom-call(s32[3]{0:T(128)} %shift_ref.1, s32[1,256]{1,0:T(1,128)} %bitcast.6, f32[3,256,128]{2,1,0:T(8,128)} %bitcast.5, s32[256,128]{1,0:T(8,128)} %cell_ref.1, s32[32,32,32]{2,1,0:T(8,128)} %rotation_ref.1), custom_call_target="tpu_custom_call" | custom-call | flops 8589934592 | bytes 2097152 | tf_op jit(solution)/shard_map/pallas_call | solution.py:452
  38.9 17.9 %shard_map.78 = (f32[12,3,32,128]{3,2,1,0:T(8,128)}, f32[3,4,8,128]{3,2,1,0:T(8,128)}) custom-call(f32[1536,128]{1,0:T(8,128)} %get-tuple-element.6.recv_ref, f32[192,128]{1,0:T(8,128)} %get-tuple-element.7.table_ref, f32[8,128]{1,0:T(8,128)} %constant.2.clone.axis_ref), custom_call_target="tpu_custom_call" | custom-call | flops 8589934592 | bytes 2097152 | tf_op jit(solution)/shard_map/pallas_call | solution.py:482

commit v2 on v1

--- a/solution.py
+++ b/solution.py
@@ -24,7 +24,8 @@
 INNER = SIDE + CX - 1
 TILES = INNER + ((CX - 1) * (CY - 1) + 1) // 2
 WIDE = 2 * CZ
-STEP = 8
+BOUND = 2 * INNER
+ROWS = BOUND + (CX - 1) * (CY - 1)
 
 angle_cosine = -0.6427876096865393
 angle_sine = 0.766044443118978
@@ -112,14 +113,25 @@
 
 def exchange_kernel(
     sizes,
+    slots,
     room,
+    shift_hbm,
+    target_hbm,
+    velocity_hbm,
+    cell_hbm,
+    rotation_hbm,
+    axis_hbm,
+    base_ref,
+    code_ref,
+    table_ref,
+    pull_ref,
     shift_ref,
     target_ref,
     velocity_ref,
     cell_ref,
     rotation_ref,
+    axis_ref,
     recv_ref,
-    table_ref,
     send_ref,
     total_ref,
     tile_ref,
@@ -127,6 +139,8 @@
     block_ref,
     plane_ref,
     kind_ref,
+    direction_ref,
+    load_sem,
     send_sem,
     recv_sem,
     halo_send_sem,
@@ -134,29 +148,54 @@
 ):
     nx, ny, nz = sizes
     devices = nx * ny * nz
+    half_y = ny // 2
     blocks = velocity_ref.shape[1]
     per = 4 * room
     place = tuple(lax.axis_index(axis) for axis in AXES)
     me = (place[0] * ny + place[1]) * nz + place[2]
 
-    def away(k, sign):
-        ox, oy, oz = k // (ny * nz), k // nz % ny, k % nz
+    loads = [
+        pltpu.make_async_copy(source, sink, load_sem.at[i])
+        for i, (source, sink) in enumerate(
+            (
+                (target_hbm, target_ref),
+                (cell_hbm, cell_ref),
+                (velocity_hbm, velocity_ref),
+                (shift_hbm, shift_ref),
+                (rotation_hbm, rotation_ref),
+                (axis_hbm, axis_ref),
+            )
+        )
+    ]
+    for load in loads:
+        load.start()
+
+    def wrap(value, size):
+        return jnp.where(value >= size, value - size, value)
+
+    low_y = place[1] % half_y
+    base_y = place[1] - low_y
+
+    def partner(k, sign):
+        q = k // 2
+        ox, oy, oz = q // (nz * half_y), q // nz % half_y, q % nz
+        if sign < 0:
+            ox, oy, oz = nx - ox, half_y - oy, nz - oz
+        other = half_y * (k % 2)
         there = (
-            (place[0] + sign * ox + nx) % nx,
-            (place[1] + sign * oy + ny) % ny,
-            (place[2] + sign * oz + nz) % nz,
+            wrap(place[0] + ox, nx),
+            wrap(base_y + other, ny) + wrap(low_y + oy, half_y),
+            wrap(place[2] + oz, nz),
         )
         return there, (there[0] * ny + there[1]) * nz + there[2]
 
     barrier = pltpu.get_barrier_semaphore()
-
-    def greet(k, carry):
-        there, number = away(k, 1)
-        pl.semaphore_signal(barrier, inc=1, device_id=there, device_id_type=MESH_ID)
-        return carry
-
-    lax.fori_loop(1, devices, greet, 0)
-
+    for k in range(1, devices):
+        pl.semaphore_signal(
+            barrier, inc=1, device_id=partner(k, 1)[0], device_id_type=MESH_ID
+        )
+
+    loads[0].wait()
     target = target_ref[...]
     named = (lax.broadcasted_iota(jnp.int32, (devices, blocks), 0) == target).astype(jnp.float32)
     earlier = (
@@ -173,7 +212,9 @@
         .astype(jnp.float32)
         .astype(jnp.bfloat16)
     )
+    loads[1].wait()
     codes = position_codes(cell_ref[...]).astype(jnp.float32)
+    loads[2].wait()
     for channel in range(4):
         left = codes if channel == 0 else velocity_ref[channel - 1]
         placed = None
@@ -184,6 +225,8 @@
             left = left - upper.astype(jnp.float32)
         send_ref[pl.ds(channel, devices * room, stride=4), :] = placed
 
+    for load in loads[3:]:
+        load.wait()
     lane = lax.broadcasted_iota(jnp.int32, (APER, 128), 1)
     depth_index = (lane + place[2] * CZ + shift_ref[2]) % APER
     for ex in range(CX + 1):
@@ -196,7 +239,7 @@
             row = block_ref[pl.ds(ex * APER + index_y, 1), :]
             plane_ref[ex * EY + ey : ex * EY + ey + 1, :] = row
             at = row_of_plane(ex, ey)
-            kind_ref[at // 2, at % 2 : at % 2 + 1, :] = row
+            kind_ref[at : at + 1, :] = row
     planes = plane_ref[0 : 8 * (PLANES // 8 + 1), :]
     sublane = lax.broadcasted_iota(jnp.int32, planes.shape, 0)
     lanes = lax.broadcasted_iota(jnp.int32, planes.shape, 1)
@@ -204,14 +247,19 @@
     rim_kind = jnp.sum(
         jnp.where((sublane == lanes) & (sublane < PLANES), first, 0.0), axis=0, keepdims=True
     )
-    kind_ref[RIM, 0:1, :] = rim_kind
-    kind_ref[RIM, 1:2, :] = rim_kind
-    kind_ref[TILES - 1, 1:2, :] = jnp.zeros((1, 128), jnp.float32)
+    kind_ref[2 * RIM : 2 * RIM + 1, :] = rim_kind
+    kind_ref[2 * RIM + 1 : 2 * RIM + 2, :] = rim_kind
+    kind_ref[ROWS : 2 * TILES, :] = jnp.zeros((2 * TILES - ROWS, 128), jnp.float32)
+    kinds = kind_ref[...].astype(jnp.int32)
+    for component in range(3):
+        direction_ref[component] = take_lanes(
+            jnp.broadcast_to(axis_ref[component : component + 1, :], kinds.shape), kinds
+        )
 
     pl.semaphore_wait(barrier, devices - 1)
 
     def outgoing(k):
-        there, number = away(k, 1)
+        there, number = partner(k, 1)
         return pltpu.make_async_remote_copy(
             src_ref=send_ref.at[pl.ds(pl.multiple_of(number * per, 8), per), :],
             dst_ref=recv_ref.at[pl.ds(pl.multiple_of(me * per, 8), per), :],
@@ -221,18 +269,27 @@
             device_id_type=MESH_ID,
         )
 
-    def start(k, carry):
+    for k in range(1, devices):
         outgoing(k).start()
-        return carry
-
-    lax.fori_loop(1, devices, start, 0)
     own = pl.ds(pl.multiple_of(me * per, 8), per)
     recv_ref[own, :] = send_ref[own, :]
     total_ref[...] = jnp.zeros(total_ref.shape, jnp.float32)
     half = lax.broadcasted_iota(jnp.int32, (8, 128), 0)
 
+    def select_rows(source, rows, row, lane, channels, start):
+        found = [jnp.zeros(row.shape, jnp.float32) for c in range(channels)]
+        for r in rows:
+            here = row == r
+            for c in range(channels):
+                at = start(r, c)
+                line = jnp.broadcast_to(source[at : at + 1, :], row.shape)
+                found[c] = jnp.where(here, take_lanes(line, lane), found[c])
+        return found
+
+    firsts = [0] if room <= 8 else [*range(0, room - 7, 8)] + ([room - 8] if room % 8 else [])
+
     def add_sender(k, carry):
-        _, number = away(k, -1)
+        _, number = partner(k, -1)
         base = pl.multiple_of(number * per, 8)
 
         @pl.when(k > 0)
@@ -274,6 +331,26 @@
                 (((1,), (1,)), ((), ())),
                 preferred_element_type=jnp.float32,
             )
+
+        for first in firsts:
+            take = min(8, room)
+
+            def rows_of(channel):
+                rows = recv_ref[pl.ds(base + 4 * first + channel, take, stride=4), :]
+                return jnp.concatenate([rows] * (8 // take), axis=0)
+
+            code = rows_of(0).astype(jnp.int32)
+            kind = select_rows(kind_ref, range(ROWS), code >> 7, code & 127, 1, lambda r, c: r)[0]
+            kind = kind.astype(jnp.int32)
+            direction = [
+                take_lanes(jnp.broadcast_to(axis_ref[c : c + 1, :], (8, 128)), kind)
+                for c in range(3)
+            ]
+            turned = rotate_about(direction, [rows_of(c + 1) for c in range(3)])
+            code_ref[pl.ds(first * devices + number, take, stride=devices), :] = code[:take]
+            for c in range(3):
+                at = (3 * first + c) * devices + number
+                base_ref[pl.ds(at, take, stride=3 * devices), :] = turned[c][:take]
         return carry
 
     lax.fori_loop(0, devices, add_sender, 0)
@@ -294,7 +371,9 @@
     copies = []
     for step in steps:
         low, high = halo_tiles(step)
-        there = tuple((p + d + size) % size for p, d, size in zip(place, step, sizes))
+        there = tuple(
+            wrap(p + d % size, size) if d else p for p, d, size in zip(place, step, sizes)
+        )
         landing = slot_of(tuple(-d for d in step))
         copies.append(
             pltpu.make_async_remote_copy(
@@ -309,11 +388,43 @@
     for copy in copies:
         copy.start()
 
-    def sent(k, carry):
+    def both(low, high):
+        return jnp.where(half < 4, low, high)
+
+    def finish(tile, value):
+        count = both(
+            jnp.broadcast_to(value[0:1], (8, 128)), jnp.broadcast_to(value[4:5], (8, 128))
+        )
+        table_ref[8 * tile : 8 * tile + 8, :] = value / jnp.maximum(count, 1.0)
+
+    def pulls(low, high):
+        mean = [table_ref[pl.ds(4 * low + 1 + c, high - low, stride=4), :] for c in range(3)]
+        direction = [direction_ref[c, low:high, :] for c in range(3)]
+        turned = rotate_about(direction, mean)
+        for c in range(3):
+            pull_ref[pl.ds(4 * low + 1 + c, high - low, stride=4), :] = mean[c] - turned[c]
+
+    for tile in range(INNER, TILES):
+        finish(tile, tile_ref[tile])
+    pulls(BOUND, 2 * TILES)
+    groups = devices // 8
+
+    def inner(s, carry):
+        for g in range(groups):
+            at = pl.multiple_of(s * devices, 8) + 8 * g
+            code = code_ref[pl.ds(at, 8), :]
+            found = select_rows(
+                pull_ref, range(BOUND, ROWS), code >> 7, code & 127, 3, lambda r, c: 4 * r + 1 + c
+            )
+            for c in range(3):
+                place_at = pl.ds(pl.multiple_of((3 * s + c) * devices, 8) + 8 * g, 8)
+                base_ref[place_at, :] = base_ref[place_at, :] + found[c]
+        return carry
+
+    lax.fori_loop(0, slots, inner, 0)
+
+    for k in range(1, devices):
         outgoing(k).wait_send()
-        return carry
-
-    lax.fori_loop(1, devices, sent, 0)
     for copy in copies:
         copy.wait()
 
@@ -324,9 +435,6 @@
     def turned(step, tile):
         return pltpu.roll(got(step, tile), 4, 0)
 
-    def both(low, high):
-        return jnp.where(half < 4, low, high)
-
     lane = lax.broadcasted_iota(jnp.int32, (8, 128), 1)
     plane_x = (lane * 57) >> 9
     plane_y = lane - plane_x * EY
@@ -335,7 +443,7 @@
         own_rim = tile_ref[RIM] if (dx, dy) == (0, 0) else got((dx, dy, 0), RIM)
         return own_rim + both(turned((dx, dy, 1), RIM), turned((dx, dy, -1), RIM))
 
-    for tile in range(TILES):
+    for tile in range(INNER):
         value = tile_ref[tile]
         if tile < RIM or tile in (LOW, HIGH):
             value = value + both(turned((-1, 0, 0), tile), turned((1, 0, 0), tile))
@@ -358,36 +466,12 @@
                         inside = inside & (plane_y == (CY if dy > 0 else 0))
                     moved = pltpu.roll(rim(dx, dy), (dx * CX * EY + dy * CY) % 128, 1)
                     value = value + jnp.where(inside, moved, 0.0)
-        count = both(
-            jnp.broadcast_to(value[0:1], (8, 128)), jnp.broadcast_to(value[4:5], (8, 128))
-        )
-        mean = value / jnp.maximum(count, 1.0)
-        kind = both(
-            jnp.broadcast_to(kind_ref[tile, 0:1, :], (8, 128)),
-            jnp.broadcast_to(kind_ref[tile, 1:2, :], (8, 128)),
-        )
-        table_ref[8 * tile : 8 * tile + 8, :] = jnp.where(half % 4 == 0, kind, mean)
-
-
-def update_kernel(slots, room, recv_ref, table_ref, axis_ref, out_ref, flow_ref, held_ref):
+        finish(tile, value)
+    pulls(0, BOUND)
+
+
+def update_kernel(slots, base_ref, code_ref, table_ref, pull_ref, out_ref, flow_ref):
     devices = out_ref.shape[2]
-    per = 4 * room
-    groups = devices // STEP
-    for channel in range(4):
-        value = jnp.concatenate(
-            [
-                table_ref[pl.ds(channel, TILES, stride=8), :],
-                table_ref[pl.ds(channel + 4, TILES, stride=8), :],
-            ],
-            axis=1,
-        )
-        upper = value.astype(jnp.bfloat16)
-        held_ref[channel * TILES : (channel + 1) * TILES, :] = upper
-        if channel > 0:
-            held_ref[(channel + 3) * TILES : (channel + 4) * TILES, :] = (
-                value - upper.astype(jnp.float32)
-            ).astype(jnp.bfloat16)
-
     sublane = lax.broadcasted_iota(jnp.int32, (CY, 128), 0)
     lane = lax.broadcasted_iota(jnp.int32, (CY, 128), 1)
     for component in range(3):
@@ -402,42 +486,23 @@
             edge = take_lanes(rim, sublane + ex * EY)
             flow_ref[component, ex] = jnp.where(lane == 0, edge, flow)
 
-    by_row = lax.broadcasted_iota(jnp.int32, (TILES, 2 * 128), 0)
-    by_column = lax.broadcasted_iota(jnp.int32, (WIDE, 2 * 128), 0)
-
-    def step(i, carry):
-        rank = i // groups
-        sender = (i % groups) * STEP
-        blocks = [
-            recv_ref[pl.ds((sender + j) * per + 4 * rank, 4), :] for j in range(STEP)
-        ]
-        picked = [[] for channel in range(4)]
-        for j in range(0, STEP, 2):
-            code = jnp.concatenate([blocks[j][0:1], blocks[j + 1][0:1]], axis=1).astype(jnp.int32)
-            onehot = (by_column == (code & (WIDE - 1))).astype(jnp.float32).astype(jnp.bfloat16)
-            read = jnp.dot(held_ref[...], onehot, preferred_element_type=jnp.float32)
-            here = by_row == code >> 8
-            for channel in range(4):
-                value = read[channel * TILES : (channel + 1) * TILES]
-                if channel > 0:
-                    value = value + read[(channel + 3) * TILES : (channel + 4) * TILES]
-                row = jnp.sum(jnp.where(here, value, 0.0), axis=0, keepdims=True)
-                picked[channel] += [row[:, :128], row[:, 128:]]
-        held = [jnp.concatenate(rows, axis=0) for rows in picked]
-        own = [jnp.concatenate([block[c : c + 1] for block in blocks], axis=0) for c in range(4)]
-        kind = held[0].astype(jnp.int32)
-        direction = [
-            take_lanes(jnp.broadcast_to(axis_ref[c : c + 1, :], (STEP, 128)), kind)
-            for c in range(3)
-        ]
-        relative = [own[c + 1] - held[c + 1] for c in range(3)]
-        turned = rotate_about(direction, relative)
-        there = pl.ds(pl.multiple_of(sender, STEP), STEP)
-        for c in range(3):
-            out_ref[rank, c, there, :] = held[c + 1] + turned[c]
+    def outer(s, carry):
+        for g in range(devices // 8):
+            code = code_ref[pl.ds(pl.multiple_of(s * devices, 8) + 8 * g, 8), :]
+            row, depth = code >> 7, code & 127
+            found = [jnp.zeros((8, 128), jnp.float32) for c in range(3)]
+            for r in range(BOUND):
+                here = row == r
+                for c in range(3):
+                    at = 4 * r + 1 + c
+                    line = jnp.broadcast_to(pull_ref[at : at + 1, :], (8, 128))
+                    found[c] = jnp.where(here, take_lanes(line, depth), found[c])
+            for c in range(3):
+                at = pl.multiple_of((3 * s + c) * devices, 8) + 8 * g
+                out_ref[s, c, 8 * g : 8 * g + 8, :] = base_ref[pl.ds(at, 8), :] + found[c]
         return carry
 
-    lax.fori_loop(0, slots * groups, step, 0)
+    lax.fori_loop(0, slots, outer, 0)
 
 
 def shards(velocity, cell_index, block_target, rotation_axis, grid_shift):
@@ -449,22 +514,34 @@
     room = slots + slots % 2
     count = len(neighbours(sizes))
     vmem = pl.BlockSpec(memory_space=pltpu.VMEM)
-    arrived, table = pl.pallas_call(
-        functools.partial(exchange_kernel, sizes, room),
+    hbm = pl.BlockSpec(memory_space=pltpu.HBM)
+    handed = pl.pallas_call(
+        functools.partial(exchange_kernel, sizes, slots, room),
         out_shape=[
-            jax.ShapeDtypeStruct((devices * room * 4, lanes), jnp.float32),
-            jax.ShapeDtypeStruct((8 * TILES, lanes), jnp.float32),
+            pltpu.VMEM((room * 3 * devices, lanes), jnp.float32),
+            pltpu.VMEM((room * devices, lanes), jnp.int32),
+            pltpu.VMEM((8 * TILES, lanes), jnp.float32),
+            pltpu.VMEM((8 * TILES, lanes), jnp.float32),
         ],
-        in_specs=[pl.BlockSpec(memory_space=pltpu.SMEM), vmem, vmem, vmem, vmem],
-        out_specs=[vmem, vmem],
+        in_specs=[hbm] * 6,
+        out_specs=[vmem] * 4,
         scratch_shapes=[
+            pltpu.SMEM((3,), jnp.int32),
+            pltpu.VMEM((1, blocks), jnp.int32),
+            pltpu.VMEM((3, blocks, lanes), jnp.float32),
+            pltpu.VMEM((blocks, lanes), jnp.int32),
+            pltpu.VMEM((APER, APER, APER), jnp.int32),
+            pltpu.VMEM((8, 128), jnp.float32),
+            pltpu.VMEM((devices * room * 4, lanes), jnp.float32),
             pltpu.VMEM((devices * room * 4, lanes), jnp.float32),
             pltpu.VMEM((2, 8 * TILES, WIDE), jnp.float32),
             pltpu.VMEM((TILES, 8, lanes), jnp.float32),
             pltpu.VMEM((count, SIDE, 8, lanes), jnp.float32),
             pltpu.VMEM(((CX + 1) * APER, lanes), jnp.float32),
             pltpu.VMEM((8 * (PLANES // 8 + 1), lanes), jnp.float32),
-            pltpu.VMEM((TILES, 8, lanes), jnp.float32),
+            pltpu.VMEM((2 * TILES, lanes), jnp.float32),
+            pltpu.VMEM((3, 2 * TILES, lanes), jnp.float32),
+            pltpu.SemaphoreType.DMA((6,)),
             pltpu.SemaphoreType.DMA((devices,)),
             pltpu.SemaphoreType.DMA((devices,)),
             pltpu.SemaphoreType.DMA((count,)),
@@ -478,18 +555,18 @@
         jnp.transpose(velocity, (1, 0, 2)),
         cell_index,
         rotation_axis,
+        jnp.asarray(axis_rows()),
     )
     updated, flow = pl.pallas_call(
-        functools.partial(update_kernel, slots, room),
+        functools.partial(update_kernel, slots),
         out_shape=[
             jax.ShapeDtypeStruct((slots, 3, devices, lanes), jnp.float32),
             jax.ShapeDtypeStruct((3, CX, CY, CZ), jnp.float32),
         ],
-        in_specs=[vmem, vmem, vmem],
+        in_specs=[vmem] * 4,
         out_specs=[vmem, vmem],
-        scratch_shapes=[pltpu.VMEM((7 * TILES, WIDE), jnp.bfloat16)],
         cost_estimate=pl.CostEstimate(flops=1 << 33, bytes_accessed=1 << 21, transcendentals=0),
-    )(arrived, table, jnp.asarray(axis_rows()))
+    )(*[pltpu.with_memory_space_constraint(array, pltpu.VMEM) for array in handed])
     return (jnp.transpose(updated, (2, 0, 1, 3))[None], flow)
 
 

time: 56.9 us -> 43.3 us (0.76)
  Pallas kernels: 56.1 us -> 42.5 us
    pallas_call x2, Pallas kernels: 56.1 us -> 42.5 us  [the longest x1 36.6 us: shards(): pl.pallas_call(functools.partial(exchange_kernel, sizes, slots, room), ou...]
where the time goes in v2:
time: 43.3 us; the launch traced here: 43.2 us
  Pallas kernels  42.5 us (98%)
  between operations  0.64 us (1%)
    pallas_call x1, Pallas kernels, shards(): pl.pallas_call(functools.partial(exchange_kernel, sizes, slots, room), ou...  36.6 us
    pallas_call x1, Pallas kernels, shards(): pl.pallas_call(functools.partial(update_kernel, slots), out_shape=[jax.Sh...  5.89 us

profile of v2, /device:TPU:0, one launch (start us, length us, event | category | flops | bytes accessed | tf_op | source)
XLA Modules:
  0.0 43.2 jit_solution(18181970686341885774)
XLA Ops:
  0.6 36.6 %shard_map.77 = (f32[1152,128]{1,0:T(8,128)S(1)}, s32[384,128]{1,0:T(8,128)S(1)}, f32[192,128]{1,0:T(8,128)S(1)}, f32[192,128]{1,0:T(8,128)S(1)}) custom-call(s32[3]{0:T(128)} %shift_hbm.1, s32[1,256]{1,0:T(1,128)} %bitcast.6, f32[3,256,128]{2,1,0:T(8,128)} %bitcast.5, s32[256,128]{1,0:T(8,128)} %cell_hbm.1, s32[32,32,32]{2,1,0:T(8,128)} %rotation_hbm.1, ...), custom_call_target="tpu_custom_call" | custom-call | flops 8589934592 | bytes 2097152 | tf_op jit(solution)/shard_map/pallas_call | solution.py:518
  37.3 5.9 %shard_map.78 = (f32[12,3,32,128]{3,2,1,0:T(8,128)}, f32[3,4,8,128]{3,2,1,0:T(8,128)}) custom-call(f32[1152,128]{1,0:T(8,128)S(1)} %get-tuple-element.8.base_ref, s32[384,128]{1,0:T(8,128)S(1)} %get-tuple-element.9.code_ref, f32[192,128]{1,0:T(8,128)S(1)} %get-tuple-element.10.table_ref, f32[192,128]{1,0:T(8,128)S(1)} %get-tuple-element.11.pull_ref), custom_call_target="tpu_custom_call" | custom-call | flops 8589934592 | bytes 2097152 | tf_op jit(solution)/shard_map/pallas_call | solution.py:560

commit v3 on v2

--- a/solution.py
+++ b/solution.py
@@ -145,10 +145,11 @@
     recv_sem,
     halo_send_sem,
     halo_recv_sem,
+    near_sem,
+    far_sem,
 ):
     nx, ny, nz = sizes
     devices = nx * ny * nz
-    half_y = ny // 2
     blocks = velocity_ref.shape[1]
     per = 4 * room
     place = tuple(lax.axis_index(axis) for axis in AXES)
@@ -173,27 +174,52 @@
     def wrap(value, size):
         return jnp.where(value >= size, value - size, value)
 
-    low_y = place[1] % half_y
-    base_y = place[1] - low_y
+    plane = nx * nz
+    in_line = ny == 4
+    inner_plane = (place[1] == 1) | (place[1] == 2)
+    if in_line:
+        buddy = jnp.where(place[1] % 2 == 0, place[1] + 1, place[1] - 1)
+        upper_half = place[1] >= 2
+        across = [jnp.where(upper_half, 1, 2), jnp.where(upper_half, 0, 3)]
+
+    def number_of(there):
+        return (there[0] * ny + there[1]) * nz + there[2]
 
     def partner(k, sign):
-        q = k // 2
-        ox, oy, oz = q // (nz * half_y), q // nz % half_y, q % nz
+        stage, ox, oz = k // plane, k // nz % nx, k % nz
         if sign < 0:
-            ox, oy, oz = nx - ox, half_y - oy, nz - oz
-        other = half_y * (k % 2)
-        there = (
-            wrap(place[0] + ox, nx),
-            wrap(base_y + other, ny) + wrap(low_y + oy, half_y),
-            wrap(place[2] + oz, nz),
-        )
-        return there, (there[0] * ny + there[1]) * nz + there[2]
+            ox, oz = nx - ox, nz - oz
+        if in_line:
+            rows = [place[1], buddy, *across]
+            if isinstance(stage, int):
+                row = rows[stage]
+            else:
+                row = jnp.where(
+                    stage < 2,
+                    jnp.where(stage < 1, rows[0], rows[1]),
+                    jnp.where(stage < 3, rows[2], rows[3]),
+                )
+        else:
+            row = wrap(place[1] + (ny - stage if sign < 0 else stage), ny)
+        return wrap(place[0] + ox, nx), row, wrap(place[2] + oz, nz)
 
     barrier = pltpu.get_barrier_semaphore()
-    for k in range(1, devices):
-        pl.semaphore_signal(
-            barrier, inc=1, device_id=partner(k, 1)[0], device_id_type=MESH_ID
-        )
+
+    def greet(steps):
+        for k in steps:
+            pl.semaphore_signal(
+                barrier, inc=1, device_id=partner(k, 1), device_id_type=MESH_ID
+            )
+
+    if in_line:
+        greet(range(1, 2 * plane))
+
+        @pl.when(inner_plane)
+        def greet_across():
+            greet(range(2 * plane, 3 * plane))
+
+    else:
+        greet(range(1, devices))
 
     loads[0].wait()
     target = target_ref[...]
@@ -256,21 +282,55 @@
             jnp.broadcast_to(axis_ref[component : component + 1, :], kinds.shape), kinds
         )
 
-    pl.semaphore_wait(barrier, devices - 1)
-
     def outgoing(k):
-        there, number = partner(k, 1)
+        there = partner(k, 1)
+        number = number_of(there)
         return pltpu.make_async_remote_copy(
             src_ref=send_ref.at[pl.ds(pl.multiple_of(number * per, 8), per), :],
             dst_ref=recv_ref.at[pl.ds(pl.multiple_of(me * per, 8), per), :],
-            send_sem=send_sem.at[k],
-            recv_sem=recv_sem.at[k],
+            send_sem=send_sem.at[number],
+            recv_sem=recv_sem.at[me],
             device_id=there,
             device_id_type=MESH_ID,
         )
 
-    for k in range(1, devices):
-        outgoing(k).start()
+    def start(steps):
+        for k in steps:
+            outgoing(k).start()
+
+    if in_line:
+        pl.semaphore_wait(barrier, 2 * plane - 1 + jnp.where(inner_plane, plane, 0))
+
+        def tell(semaphore, row):
+            there = (place[0], row, place[2])
+            pl.semaphore_signal(semaphore, inc=1, device_id=there, device_id_type=MESH_ID)
+
+        @pl.when(inner_plane)
+        def pass_on():
+            tell(near_sem, across[0])
+            tell(near_sem, buddy)
+
+        start(range(1, 2 * plane))
+
+        @pl.when(jnp.logical_not(inner_plane))
+        def outer_hears():
+            pl.semaphore_wait(near_sem, 1)
+
+        start(range(2 * plane, 3 * plane))
+
+        @pl.when(inner_plane)
+        def inner_hears():
+            pl.semaphore_wait(near_sem, 1)
+            tell(far_sem, buddy)
+
+        @pl.when(jnp.logical_not(inner_plane))
+        def outer_hears_again():
+            pl.semaphore_wait(far_sem, 1)
+
+        start(range(3 * plane, devices))
+    else:
+        pl.semaphore_wait(barrier, devices - 1)
+        start(range(1, devices))
     own = pl.ds(pl.multiple_of(me * per, 8), per)
     recv_ref[own, :] = send_ref[own, :]
     total_ref[...] = jnp.zeros(total_ref.shape, jnp.float32)
@@ -288,21 +348,8 @@
 
     firsts = [0] if room <= 8 else [*range(0, room - 7, 8)] + ([room - 8] if room % 8 else [])
 
-    def add_sender(k, carry):
-        _, number = partner(k, -1)
-        base = pl.multiple_of(number * per, 8)
-
-        @pl.when(k > 0)
-        def arrived():
-            pltpu.make_async_remote_copy(
-                src_ref=recv_ref.at[pl.ds(base, per), :],
-                dst_ref=recv_ref.at[pl.ds(base, per), :],
-                send_sem=send_sem.at[k],
-                recv_sem=recv_sem.at[k],
-                device_id=place,
-                device_id_type=MESH_ID,
-            ).wait_recv()
-
+    def add_sender(k, part):
+        base = pl.multiple_of(number_of(partner(k, -1)) * per, 8)
         by_row = lax.broadcasted_iota(jnp.int32, (8 * TILES, 128), 0) >> 3
         by_column = lax.broadcasted_iota(jnp.int32, (WIDE, 128), 0)
         lefts, rights = [], []
@@ -323,14 +370,16 @@
                 rights.append(
                     (by_column == (code & (WIDE - 1))).astype(jnp.float32).astype(jnp.bfloat16)
                 )
-        middle = room // 2
-        for part, span in enumerate((slice(0, middle), slice(middle, room))):
-            total_ref[part] += lax.dot_general(
-                jnp.concatenate(lefts[span], axis=1),
-                jnp.concatenate(rights[span], axis=1),
-                (((1,), (1,)), ((), ())),
-                preferred_element_type=jnp.float32,
-            )
+        total_ref[part] += lax.dot_general(
+            jnp.concatenate(lefts, axis=1),
+            jnp.concatenate(rights, axis=1),
+            (((1,), (1,)), ((), ())),
+            preferred_element_type=jnp.float32,
+        )
+
+    def turn_sender(k):
+        number = number_of(partner(k, -1))
+        base = pl.multiple_of(number * per, 8)
 
         for first in firsts:
             take = min(8, room)
@@ -351,9 +400,32 @@
             for c in range(3):
                 at = (3 * first + c) * devices + number
                 base_ref[pl.ds(at, take, stride=3 * devices), :] = turned[c][:take]
+
+    def arrived(k):
+        number = number_of(partner(k, -1))
+        landing = recv_ref.at[pl.ds(pl.multiple_of(number * per, 8), per), :]
+        pltpu.make_async_remote_copy(
+            src_ref=landing,
+            dst_ref=landing,
+            send_sem=send_sem.at[number],
+            recv_sem=recv_sem.at[number],
+            device_id=place,
+            device_id_type=MESH_ID,
+        ).wait_recv()
+
+    def add_two(i, carry):
+        @pl.when(i > 0)
+        def first_arrived():
+            arrived(2 * i)
+
+        arrived(2 * i + 1)
+        for part in range(2):
+            add_sender(2 * i + part, part)
+        for part in range(2):
+            turn_sender(2 * i + part)
         return carry
 
-    lax.fori_loop(0, devices, add_sender, 0)
+    lax.fori_loop(0, devices // 2, add_two, 0)
 
     for tile in range(TILES):
         rows = pl.ds(8 * tile, 8)
@@ -546,6 +618,8 @@
             pltpu.SemaphoreType.DMA((devices,)),
             pltpu.SemaphoreType.DMA((count,)),
             pltpu.SemaphoreType.DMA((count,)),
+            pltpu.SemaphoreType.REGULAR,
+            pltpu.SemaphoreType.REGULAR,
         ],
         compiler_params=pltpu.CompilerParams(collective_id=0, has_side_effects=True),
         cost_estimate=pl.CostEstimate(flops=1 << 33, bytes_accessed=1 << 21, transcendentals=0),

time: 43.3 us -> 42.7 us (0.986)
  Pallas kernels: 42.5 us -> 41.9 us
    pallas_call x1, Pallas kernels: 36.6 us -> 36 us  [shards(): pl.pallas_call(functools.partial(exchange_kernel, sizes, slots, room), ou...]
where the time goes in v3:
time: 42.7 us; the launch traced here: 42.6 us
  Pallas kernels  41.9 us (98%)
  between operations  0.64 us (1%)
    pallas_call x1, Pallas kernels, shards(): pl.pallas_call(functools.partial(exchange_kernel, sizes, slots, room), ou...  36 us
    pallas_call x1, Pallas kernels, shards(): pl.pallas_call(functools.partial(update_kernel, slots), out_shape=[jax.Sh...  5.89 us

profile of v3, /device:TPU:0, one launch (start us, length us, event | category | flops | bytes accessed | tf_op | source)
XLA Modules:
  0.0 42.6 jit_solution(5700937767279200127)
XLA Ops:
  0.6 36.0 %shard_map.77 = (f32[1152,128]{1,0:T(8,128)S(1)}, s32[384,128]{1,0:T(8,128)S(1)}, f32[192,128]{1,0:T(8,128)S(1)}, f32[192,128]{1,0:T(8,128)S(1)}) custom-call(s32[3]{0:T(128)} %shift_hbm.1, s32[1,256]{1,0:T(1,128)} %bitcast.6, f32[3,256,128]{2,1,0:T(8,128)} %bitcast.5, s32[256,128]{1,0:T(8,128)} %cell_hbm.1, s32[32,32,32]{2,1,0:T(8,128)} %rotation_hbm.1, ...), custom_call_target="tpu_custom_call" | custom-call | flops 8589934592 | bytes 2097152 | tf_op jit(solution)/shard_map/pallas_call | solution.py:590
  36.7 5.9 %shard_map.78 = (f32[12,3,32,128]{3,2,1,0:T(8,128)}, f32[3,4,8,128]{3,2,1,0:T(8,128)}) custom-call(f32[1152,128]{1,0:T(8,128)S(1)} %get-tuple-element.8.base_ref, s32[384,128]{1,0:T(8,128)S(1)} %get-tuple-element.9.code_ref, f32[192,128]{1,0:T(8,128)S(1)} %get-tuple-element.10.table_ref, f32[192,128]{1,0:T(8,128)S(1)} %get-tuple-element.11.pull_ref), custom_call_target="tpu_custom_call" | custom-call | flops 8589934592 | bytes 2097152 | tf_op jit(solution)/shard_map/pallas_call | solution.py:634

commit v4 on v3

--- a/solution.py
+++ b/solution.py
@@ -26,6 +26,8 @@
 WIDE = 2 * CZ
 BOUND = 2 * INNER
 ROWS = BOUND + (CX - 1) * (CY - 1)
+AHEAD = 2
+SHARE = 4
 
 angle_cosine = -0.6427876096865393
 angle_sine = 0.766044443118978
@@ -140,6 +142,7 @@
     plane_ref,
     kind_ref,
     direction_ref,
+    held_ref,
     load_sem,
     send_sem,
     recv_sem,
@@ -221,7 +224,8 @@
     else:
         greet(range(1, devices))
 
-    loads[0].wait()
+    for load in loads[:3]:
+        load.wait()
     target = target_ref[...]
     named = (lax.broadcasted_iota(jnp.int32, (devices, blocks), 0) == target).astype(jnp.float32)
     earlier = (
@@ -238,18 +242,68 @@
         .astype(jnp.float32)
         .astype(jnp.bfloat16)
     )
-    loads[1].wait()
     codes = position_codes(cell_ref[...]).astype(jnp.float32)
-    loads[2].wait()
-    for channel in range(4):
-        left = codes if channel == 0 else velocity_ref[channel - 1]
+    lanes = codes.shape[1]
+    for channel, pair in ((2, (1, 2)), (0, (None, 0))):
+        left = jnp.concatenate([codes if c is None else velocity_ref[c] for c in pair], axis=1)
         placed = None
         for part in range(3):
             upper = left.astype(jnp.bfloat16)
             moved = jnp.dot(chosen, upper, preferred_element_type=jnp.float32)
             placed = moved if placed is None else placed + moved
             left = left - upper.astype(jnp.float32)
-        send_ref[pl.ds(channel, devices * room, stride=4), :] = placed
+        send_ref[pl.ds(channel, devices * room, stride=4), :] = placed[:, :lanes]
+        send_ref[pl.ds(channel + 1, devices * room, stride=4), :] = placed[:, lanes:]
+
+    def outgoing(k):
+        there = partner(k, 1)
+        number = number_of(there)
+        return pltpu.make_async_remote_copy(
+            src_ref=send_ref.at[pl.ds(pl.multiple_of(number * per, 8), per), :],
+            dst_ref=recv_ref.at[pl.ds(pl.multiple_of(me * per, 8), per), :],
+            send_sem=send_sem.at[number],
+            recv_sem=recv_sem.at[me],
+            device_id=there,
+            device_id_type=MESH_ID,
+        )
+
+    def start(steps):
+        for k in steps:
+            outgoing(k).start()
+
+    if in_line:
+        pl.semaphore_wait(barrier, 2 * plane - 1 + jnp.where(inner_plane, plane, 0))
+
+        def tell(semaphore, row):
+            there = (place[0], row, place[2])
+            pl.semaphore_signal(semaphore, inc=1, device_id=there, device_id_type=MESH_ID)
+
+        @pl.when(inner_plane)
+        def pass_on():
+            tell(near_sem, across[0])
+            tell(near_sem, buddy)
+
+        start(range(1, 2 * plane))
+
+        @pl.when(jnp.logical_not(inner_plane))
+        def outer_hears():
+            pl.semaphore_wait(near_sem, 1)
+
+        start(range(2 * plane, 2 * plane + AHEAD))
+
+        @pl.when(inner_plane)
+        def inner_hears():
+            pl.semaphore_wait(near_sem, 1)
+            tell(far_sem, buddy)
+
+        @pl.when(jnp.logical_not(inner_plane))
+        def outer_hears_again():
+            pl.semaphore_wait(far_sem, 1)
+
+        start(range(3 * plane, 3 * plane + AHEAD))
+    else:
+        pl.semaphore_wait(barrier, devices - 1)
+        start(range(1, devices))
 
     for load in loads[3:]:
         load.wait()
@@ -282,58 +336,10 @@
             jnp.broadcast_to(axis_ref[component : component + 1, :], kinds.shape), kinds
         )
 
-    def outgoing(k):
-        there = partner(k, 1)
-        number = number_of(there)
-        return pltpu.make_async_remote_copy(
-            src_ref=send_ref.at[pl.ds(pl.multiple_of(number * per, 8), per), :],
-            dst_ref=recv_ref.at[pl.ds(pl.multiple_of(me * per, 8), per), :],
-            send_sem=send_sem.at[number],
-            recv_sem=recv_sem.at[me],
-            device_id=there,
-            device_id_type=MESH_ID,
-        )
-
-    def start(steps):
-        for k in steps:
-            outgoing(k).start()
-
-    if in_line:
-        pl.semaphore_wait(barrier, 2 * plane - 1 + jnp.where(inner_plane, plane, 0))
-
-        def tell(semaphore, row):
-            there = (place[0], row, place[2])
-            pl.semaphore_signal(semaphore, inc=1, device_id=there, device_id_type=MESH_ID)
-
-        @pl.when(inner_plane)
-        def pass_on():
-            tell(near_sem, across[0])
-            tell(near_sem, buddy)
-
-        start(range(1, 2 * plane))
-
-        @pl.when(jnp.logical_not(inner_plane))
-        def outer_hears():
-            pl.semaphore_wait(near_sem, 1)
-
-        start(range(2 * plane, 3 * plane))
-
-        @pl.when(inner_plane)
-        def inner_hears():
-            pl.semaphore_wait(near_sem, 1)
-            tell(far_sem, buddy)
-
-        @pl.when(jnp.logical_not(inner_plane))
-        def outer_hears_again():
-            pl.semaphore_wait(far_sem, 1)
-
-        start(range(3 * plane, devices))
-    else:
-        pl.semaphore_wait(barrier, devices - 1)
-        start(range(1, devices))
     own = pl.ds(pl.multiple_of(me * per, 8), per)
     recv_ref[own, :] = send_ref[own, :]
     total_ref[...] = jnp.zeros(total_ref.shape, jnp.float32)
+    pull_ref[...] = jnp.zeros(pull_ref.shape, jnp.float32)
     half = lax.broadcasted_iota(jnp.int32, (8, 128), 0)
 
     def select_rows(source, rows, row, lane, channels, start):
@@ -414,15 +420,30 @@
         ).wait_recv()
 
     def add_two(i, carry):
+        pair = [2 * i, 2 * i + 1]
+        if in_line:
+            group = i // 2
+
+            @pl.when((i % 2 == 0) & (group + AHEAD < plane))
+            def start_more():
+                for stage in (2, 3):
+                    outgoing(stage * plane + group).wait_send()
+                    outgoing(stage * plane + group + AHEAD).start()
+
+            pair = [
+                jnp.where(i < plane, near, far)
+                for near, far in zip(pair, (plane + i, 2 * plane + i))
+            ]
+
         @pl.when(i > 0)
         def first_arrived():
-            arrived(2 * i)
-
-        arrived(2 * i + 1)
+            arrived(pair[0])
+
+        arrived(pair[1])
         for part in range(2):
-            add_sender(2 * i + part, part)
+            add_sender(pair[part], part)
         for part in range(2):
-            turn_sender(2 * i + part)
+            turn_sender(pair[part])
         return carry
 
     lax.fori_loop(0, devices // 2, add_two, 0)
@@ -476,36 +497,93 @@
         for c in range(3):
             pull_ref[pl.ds(4 * low + 1 + c, high - low, stride=4), :] = mean[c] - turned[c]
 
-    for tile in range(INNER, TILES):
-        finish(tile, tile_ref[tile])
-    pulls(BOUND, 2 * TILES)
+    def got(step, tile):
+        low, high = halo_tiles(step)
+        return halo_ref[slot_of(step), tile - low]
+
+    def turned(step, tile):
+        return pltpu.roll(got(step, tile), 4, 0)
+
     groups = devices // 8
 
-    def inner(s, carry):
+    def read_by_lanes(s, low, high):
         for g in range(groups):
             at = pl.multiple_of(s * devices, 8) + 8 * g
             code = code_ref[pl.ds(at, 8), :]
             found = select_rows(
-                pull_ref, range(BOUND, ROWS), code >> 7, code & 127, 3, lambda r, c: 4 * r + 1 + c
+                pull_ref, range(low, high), code >> 7, code & 127, 3, lambda r, c: 4 * r + 1 + c
             )
             for c in range(3):
-                place_at = pl.ds(pl.multiple_of((3 * s + c) * devices, 8) + 8 * g, 8)
-                base_ref[place_at, :] = base_ref[place_at, :] + found[c]
-        return carry
-
-    lax.fori_loop(0, slots, inner, 0)
-
+                there = pl.ds(pl.multiple_of((3 * s + c) * devices, 8) + 8 * g, 8)
+                base_ref[there, :] = base_ref[there, :] + found[c]
+
+    def read_by_matrix(s, first, count):
+        by_row = lax.broadcasted_iota(jnp.int32, (count, 256), 0) + first
+        by_column = lax.broadcasted_iota(jnp.int32, (WIDE, 256), 0)
+        for g in range(groups):
+            at = pl.multiple_of(s * devices, 8) + 8 * g
+            code = code_ref[pl.ds(at, 8), :]
+            found = [[], [], []]
+            for block in range(0, 8, 2):
+                label = jnp.concatenate([code[block : block + 1], code[block + 1 : block + 2]], axis=1)
+                onehot = (by_column == (label & (WIDE - 1))).astype(jnp.float32).astype(jnp.bfloat16)
+                read = jnp.dot(
+                    held_ref[0 : 6 * count, :], onehot, preferred_element_type=jnp.float32
+                )
+                here = by_row == label >> 8
+                for c in range(3):
+                    value = read[c * count : (c + 1) * count] + read[(c + 3) * count : (c + 4) * count]
+                    line = jnp.sum(jnp.where(here, value, 0.0), axis=0, keepdims=True)
+                    found[c] += [line[:, :128], line[:, 128:]]
+            for c in range(3):
+                there = pl.ds(pl.multiple_of((3 * s + c) * devices, 8) + 8 * g, 8)
+                base_ref[there, :] = base_ref[there, :] + jnp.concatenate(found[c], axis=0)
+
+    def read_rows(low, high, first, count):
+        for c in range(3):
+            value = jnp.concatenate(
+                [
+                    pull_ref[pl.ds(8 * first + 1 + c, count, stride=8), :],
+                    pull_ref[pl.ds(8 * first + 5 + c, count, stride=8), :],
+                ],
+                axis=1,
+            )
+            upper = value.astype(jnp.bfloat16)
+            held_ref[c * count : (c + 1) * count, :] = upper
+            held_ref[(c + 3) * count : (c + 4) * count, :] = (
+                value - upper.astype(jnp.float32)
+            ).astype(jnp.bfloat16)
+
+        def step(i, carry):
+            read_by_matrix(SHARE * i, first, count)
+            for other in range(1, SHARE):
+                read_by_lanes(SHARE * i + other, low, high)
+            return carry
+
+        lax.fori_loop(0, slots // SHARE, step, 0)
+        for s in range(slots - slots % SHARE, slots):
+            read_by_lanes(s, low, high)
+
+    for tile in range(INNER, TILES):
+        finish(tile, tile_ref[tile])
+    pulls(BOUND, 2 * TILES)
+    read_rows(BOUND, ROWS, TILES - 16, 16)
+    for step, copy in zip(steps, copies):
+        if step[1:] == (0, 0):
+            copy.wait()
+    for tile in range(RIM):
+        finish(
+            tile,
+            tile_ref[tile] + both(turned((-1, 0, 0), tile), turned((1, 0, 0), tile)),
+        )
+    pulls(0, 2 * RIM)
+    read_rows(0, 2 * RIM, 0, 8)
+    for step, copy in zip(steps, copies):
+        if step[1:] != (0, 0):
+            copy.wait()
     for k in range(1, devices):
-        outgoing(k).wait_send()
-    for copy in copies:
-        copy.wait()
-
-    def got(step, tile):
-        low, high = halo_tiles(step)
-        return halo_ref[slot_of(step), tile - low]
-
-    def turned(step, tile):
-        return pltpu.roll(got(step, tile), 4, 0)
+        if not (in_line and k >= 2 * plane and k % plane + AHEAD < plane):
+            outgoing(k).wait_send()
 
     lane = lax.broadcasted_iota(jnp.int32, (8, 128), 1)
     plane_x = (lane * 57) >> 9
@@ -515,9 +593,9 @@
         own_rim = tile_ref[RIM] if (dx, dy) == (0, 0) else got((dx, dy, 0), RIM)
         return own_rim + both(turned((dx, dy, 1), RIM), turned((dx, dy, -1), RIM))
 
-    for tile in range(INNER):
+    for tile in range(RIM, INNER):
         value = tile_ref[tile]
-        if tile < RIM or tile in (LOW, HIGH):
+        if tile in (LOW, HIGH):
             value = value + both(turned((-1, 0, 0), tile), turned((1, 0, 0), tile))
         if tile in (LOW, HIGH):
             dy, other = (-1, HIGH) if tile == LOW else (1, LOW)
@@ -539,7 +617,7 @@
                     moved = pltpu.roll(rim(dx, dy), (dx * CX * EY + dy * CY) % 128, 1)
                     value = value + jnp.where(inside, moved, 0.0)
         finish(tile, value)
-    pulls(0, BOUND)
+    pulls(2 * RIM, BOUND)
 
 
 def update_kernel(slots, base_ref, code_ref, table_ref, pull_ref, out_ref, flow_ref):
@@ -563,7 +641,7 @@
             code = code_ref[pl.ds(pl.multiple_of(s * devices, 8) + 8 * g, 8), :]
             row, depth = code >> 7, code & 127
             found = [jnp.zeros((8, 128), jnp.float32) for c in range(3)]
-            for r in range(BOUND):
+            for r in range(2 * RIM, BOUND):
                 here = row == r
                 for c in range(3):
                     at = 4 * r + 1 + c
@@ -613,6 +691,7 @@
             pltpu.VMEM((8 * (PLANES // 8 + 1), lanes), jnp.float32),
             pltpu.VMEM((2 * TILES, lanes), jnp.float32),
             pltpu.VMEM((3, 2 * TILES, lanes), jnp.float32),
+            pltpu.VMEM((6 * 16, WIDE), jnp.bfloat16),
             pltpu.SemaphoreType.DMA((6,)),
             pltpu.SemaphoreType.DMA((devices,)),
             pltpu.SemaphoreType.DMA((devices,)),

time: 42.7 us -> 39.4 us (0.923)
  Pallas kernels: 41.9 us -> 38.6 us
    pallas_call x1, Pallas kernels: 5.89 us -> 3.72 us  [shards(): pl.pallas_call(functools.partial(update_kernel, slots), out_shape=[jax.Sh...]
    pallas_call x1, Pallas kernels: 36 us -> 34.9 us  [shards(): pl.pallas_call(functools.partial(exchange_kernel, sizes, slots, room), ou...]
where the time goes in v4:
time: 39.4 us; the launch traced here: 39.3 us
  Pallas kernels  38.6 us (98%)
  between operations  0.64 us (2%)
    pallas_call x1, Pallas kernels, shards(): pl.pallas_call(functools.partial(exchange_kernel, sizes, slots, room), ou...  34.9 us
    pallas_call x1, Pallas kernels, shards(): pl.pallas_call(functools.partial(update_kernel, slots), out_shape=[jax.Sh...  3.72 us

profile of v4, /device:TPU:0, one launch (start us, length us, event | category | flops | bytes accessed | tf_op | source)
XLA Modules:
  0.0 39.3 jit_solution(1820234918383684133)
XLA Ops:
  0.6 34.9 %shard_map.77 = (f32[1152,128]{1,0:T(8,128)S(1)}, s32[384,128]{1,0:T(8,128)S(1)}, f32[192,128]{1,0:T(8,128)S(1)}, f32[192,128]{1,0:T(8,128)S(1)}) custom-call(s32[3]{0:T(128)} %shift_hbm.1, s32[1,256]{1,0:T(1,128)} %bitcast.6, f32[3,256,128]{2,1,0:T(8,128)} %bitcast.5, s32[256,128]{1,0:T(8,128)} %cell_hbm.1, s32[32,32,32]{2,1,0:T(8,128)} %rotation_hbm.1, ...), custom_call_target="tpu_custom_call" | custom-call | flops 8589934592 | bytes 2097152 | tf_op jit(solution)/shard_map/pallas_call | solution.py:668
  35.5 3.7 %shard_map.78 = (f32[12,3,32,128]{3,2,1,0:T(8,128)}, f32[3,4,8,128]{3,2,1,0:T(8,128)}) custom-call(f32[1152,128]{1,0:T(8,128)S(1)} %get-tuple-element.8.base_ref, s32[384,128]{1,0:T(8,128)S(1)} %get-tuple-element.9.code_ref, f32[192,128]{1,0:T(8,128)S(1)} %get-tuple-element.10.table_ref, f32[192,128]{1,0:T(8,128)S(1)} %get-tuple-element.11.pull_ref), custom_call_target="tpu_custom_call" | custom-call | flops 8589934592 | bytes 2097152 | tf_op jit(solution)/shard_map/pallas_call | solution.py:713

commit v5 on v4

--- a/solution.py
+++ b/solution.py
@@ -26,7 +26,7 @@
 WIDE = 2 * CZ
 BOUND = 2 * INNER
 ROWS = BOUND + (CX - 1) * (CY - 1)
-AHEAD = 2
+AHEAD = 3
 SHARE = 4
 
 angle_cosine = -0.6427876096865393
@@ -171,7 +171,7 @@
             )
         )
     ]
-    for load in loads:
+    for load in loads[:3]:
         load.start()
 
     def wrap(value, size):
@@ -226,6 +226,8 @@
 
     for load in loads[:3]:
         load.wait()
+    for load in loads[3:]:
+        load.start()
     target = target_ref[...]
     named = (lax.broadcasted_iota(jnp.int32, (devices, blocks), 0) == target).astype(jnp.float32)
     earlier = (

time: 39.4 us -> 38 us (0.964)
  Pallas kernels: 38.6 us -> 37.2 us
    pallas_call x1, Pallas kernels: 34.9 us -> 33.5 us  [shards(): pl.pallas_call(functools.partial(exchange_kernel, sizes, slots, room), ou...]
where the time goes in v5:
time: 38 us; the launch traced here: 37.8 us
  Pallas kernels  37.2 us (98%)
  between operations  0.64 us (2%)
    pallas_call x1, Pallas kernels, shards(): pl.pallas_call(functools.partial(exchange_kernel, sizes, slots, room), ou...  33.5 us
    pallas_call x1, Pallas kernels, shards(): pl.pallas_call(functools.partial(update_kernel, slots), out_shape=[jax.Sh...  3.72 us

profile of v5, /device:TPU:0, one launch (start us, length us, event | category | flops | bytes accessed | tf_op | source)
XLA Modules:
  0.0 37.8 jit_solution(16063377950970705384)
XLA Ops:
  0.6 33.5 %shard_map.77 = (f32[1152,128]{1,0:T(8,128)S(1)}, s32[384,128]{1,0:T(8,128)S(1)}, f32[192,128]{1,0:T(8,128)S(1)}, f32[192,128]{1,0:T(8,128)S(1)}) custom-call(s32[3]{0:T(128)} %shift_hbm.1, s32[1,256]{1,0:T(1,128)} %bitcast.6, f32[3,256,128]{2,1,0:T(8,128)} %bitcast.5, s32[256,128]{1,0:T(8,128)} %cell_hbm.1, s32[32,32,32]{2,1,0:T(8,128)} %rotation_hbm.1, ...), custom_call_target="tpu_custom_call" | custom-call | flops 8589934592 | bytes 2097152 | tf_op jit(solution)/shard_map/pallas_call | solution.py:670
  34.1 3.7 %shard_map.78 = (f32[12,3,32,128]{3,2,1,0:T(8,128)}, f32[3,4,8,128]{3,2,1,0:T(8,128)}) custom-call(f32[1152,128]{1,0:T(8,128)S(1)} %get-tuple-element.8.base_ref, s32[384,128]{1,0:T(8,128)S(1)} %get-tuple-element.9.code_ref, f32[192,128]{1,0:T(8,128)S(1)} %get-tuple-element.10.table_ref, f32[192,128]{1,0:T(8,128)S(1)} %get-tuple-element.11.pull_ref), custom_call_target="tpu_custom_call" | custom-call | flops 8589934592 | bytes 2097152 | tf_op jit(solution)/shard_map/pallas_call | solution.py:715

commit v6 on v5

--- a/solution.py
+++ b/solution.py
@@ -27,7 +27,7 @@
 BOUND = 2 * INNER
 ROWS = BOUND + (CX - 1) * (CY - 1)
 AHEAD = 3
-SHARE = 4
+SHARE = 6
 
 angle_cosine = -0.6427876096865393
 angle_sine = 0.766044443118978
@@ -285,8 +285,6 @@
             tell(near_sem, across[0])
             tell(near_sem, buddy)
 
-        start(range(1, 2 * plane))
-
         @pl.when(jnp.logical_not(inner_plane))
         def outer_hears():
             pl.semaphore_wait(near_sem, 1)
@@ -303,6 +301,7 @@
             pl.semaphore_wait(far_sem, 1)
 
         start(range(3 * plane, 3 * plane + AHEAD))
+        start(range(1, 2 * plane))
     else:
         pl.semaphore_wait(barrier, devices - 1)
         start(range(1, devices))

time: 38 us -> 38.2 us (level)
  no operation moved by 1% of the time
where the time goes in v6:
time: 38.2 us; the launch traced here: 38 us
  Pallas kernels  37.4 us (98%)
  between operations  0.64 us (2%)
    pallas_call x1, Pallas kernels, shards(): pl.pallas_call(functools.partial(exchange_kernel, sizes, slots, room), ou...  33.7 us
    pallas_call x1, Pallas kernels, shards(): pl.pallas_call(functools.partial(update_kernel, slots), out_shape=[jax.Sh...  3.72 us

profile of v6, /device:TPU:0, one launch (start us, length us, event | category | flops | bytes accessed | tf_op | source)
XLA Modules:
  0.0 38.0 jit_solution(16306036113065037424)
XLA Ops:
  0.6 33.7 %shard_map.77 = (f32[1152,128]{1,0:T(8,128)S(1)}, s32[384,128]{1,0:T(8,128)S(1)}, f32[192,128]{1,0:T(8,128)S(1)}, f32[192,128]{1,0:T(8,128)S(1)}) custom-call(s32[3]{0:T(128)} %shift_hbm.1, s32[1,256]{1,0:T(1,128)} %bitcast.6, f32[3,256,128]{2,1,0:T(8,128)} %bitcast.5, s32[256,128]{1,0:T(8,128)} %cell_hbm.1, s32[32,32,32]{2,1,0:T(8,128)} %rotation_hbm.1, ...), custom_call_target="tpu_custom_call" | custom-call | flops 8589934592 | bytes 2097152 | tf_op jit(solution)/shard_map/pallas_call | solution.py:669
  34.3 3.7 %shard_map.78 = (f32[12,3,32,128]{3,2,1,0:T(8,128)}, f32[3,4,8,128]{3,2,1,0:T(8,128)}) custom-call(f32[1152,128]{1,0:T(8,128)S(1)} %get-tuple-element.8.base_ref, s32[384,128]{1,0:T(8,128)S(1)} %get-tuple-element.9.code_ref, f32[192,128]{1,0:T(8,128)S(1)} %get-tuple-element.10.table_ref, f32[192,128]{1,0:T(8,128)S(1)} %get-tuple-element.11.pull_ref), custom_call_target="tpu_custom_call" | custom-call | flops 8589934592 | bytes 2097152 | tf_op jit(solution)/shard_map/pallas_call | solution.py:714
